TPU v7x, 128 devices: a whole 4x4x4 slice. The times are simulated.
128 devices in a mesh: gx: 4 (over z), gy: 32 (over y, x, core).
Axes of the slice: x: 4, y: 4, z: 4, core: 2. Of those that a mesh axis runs over, the one named last changes fastest.
Arguments:
- a_blocks: float32 [1024, 4, 128, 128], P(('gx', 'gy')), may hold values from -0.25 to 0.25
- a_cols: int32 [1024, 4], replicated, may hold values from 0 to 1023, as said below
- t_blocks: float32 [1024, 128, 128], P(('gx', 'gy')), may hold values from -0.5 to 0.5
- t_agg: int32 [1024], replicated, may hold values from 0 to 1, as said below
- dinv: float32 [1024, 128, 128], P(('gx', 'gy')), may hold values from -0.5 to 0.5
- coarse_inv: float32 [256, 128, 128], P(('gx', 'gy')), may hold values from -1.5 to 1.5
Outputs:
- coarse: float32 [256, 14, 128, 128], P(('gx', 'gy'))
Inputs may be any that keep to these rules, and one draw needn't show every extreme that they name: `a_cols`: block column 0 of row g is g itself; column 1 lies in g's own slab; column 2 lies in the slab below (on the cycle) and column 3 in the slab above; over the rows of one slab, columns 2 name exactly 4 distinct rows of the slab below, and columns 3 exactly 4 distinct rows of the slab above. `t_agg`: every slab's 2 aggregates each hold 4 of its rows.
All inputs are finite; a program needn't handle non-finite values.
Results may differ from a plain program's by a relative error of at most 0.0001.
Values sent between devices are 32-bit elements; how exact they have to be, the bound alone decides.
No kernel may reach another device: no remote copies, remote signals or barrier semaphores. Data moves between devices by JAX's collectives and lax.ppermute only.
A program may use at most 64 MiB of HBM per device.

v0:
```python
import functools

import jax
import jax.numpy as jnp
from jax import lax
from jax.experimental import pallas as pl
from jax.experimental.pallas import tpu as pltpu
from jax.sharding import PartitionSpec as P


OMEGA = 0.6
AXES = ("gx", "gy")
F32 = jnp.float32
BF16 = jnp.bfloat16
ROW, NEAR, POS2, POS3, LIST_0, OWN_LAB, SIDE_LAB, BACK, TAB = 0, 8, 16, 24, 32, 40, 72, 88, 96
LANES = 128
BELOW, ABOVE = 0, 1
ROW_CHUNK = 128


def exchanged(value, first):
    count = lax.axis_size(AXES)
    pairs = []
    for low in range(first, count + first, 2):
        high = (low + 1) % count
        pairs += [(low, high), (high, low)]
    return lax.ppermute(value, AXES, pairs)


def pair_side():
    return 1 - lax.rem(lax.axis_index("gy"), 2)


def split(x):
    high = x.astype(BF16)
    return high, (x - high.astype(F32)).astype(BF16)


def dot(a, b):
    return jnp.dot(a, b, preferred_element_type=F32)


def dot3(a_high, a_low, b_high, b_low):
    return dot(a_high, b_high) + dot(a_low, b_high) + dot(a_high, b_low)


def dot3k(a_high, a_low, b_high, b_low):
    both = jnp.concatenate([a_high, a_low], axis=1)
    return dot(both, jnp.concatenate([b_high, b_high], axis=0)) + dot(a_high, b_low)


def note(tab, i, value):
    tab[pl.ds(i, 1), :] = jnp.full((1, tab.shape[1]), value, jnp.int32)


def entry(tab, i):
    return tab[pl.ds(i, 1), :][0, 0]


def far_partner():
    return lax.axis_index("gy") == 0


def load_kernel(
    devices, cols_hbm, agg_hbm, t_hbm, dinv_hbm, a_hbm,
    tab, t_0, t_1, t, near_0, near_1, own, a_high, a_low, a01_high, a01_low,
    cols, agg, rank, dinv, a, sem,
):
    early = [
        pltpu.make_async_copy(dinv_hbm, dinv, sem.at[5]),
        pltpu.make_async_copy(a_hbm, a, sem.at[6]),
    ]

    rows, width = t.shape[0], t.shape[0] // 2
    device = lax.axis_index("gx") * lax.axis_size("gy") + lax.axis_index("gy")
    previous = lax.rem(device + devices - 1, devices)
    following = lax.rem(device + 1, devices)
    slabs = previous, following, device
    side = pair_side()
    shift = ROW_CHUNK.bit_length() - 1
    chunk = 4 * ROW_CHUNK
    copies = [
        pltpu.make_async_copy(
            cols_hbm.at[pl.ds(pl.multiple_of(((slab * rows) >> shift) * chunk, chunk), chunk)],
            cols.at[pl.ds(i * chunk, chunk)],
            sem.at[i],
        )
        for i, slab in enumerate(slabs)
    ]
    copies += [pltpu.make_async_copy(t_hbm, t, sem.at[3]), pltpu.make_async_copy(agg_hbm, agg, sem.at[4])]
    for i, copy in enumerate(copies):
        copy.start(priority=1 if i == 3 else 0)

    def col(i, r, k):
        return cols[i * chunk + k * ROW_CHUNK + ((slabs[i] * rows) & (ROW_CHUNK - 1)) + r]

    def rank_rows(i, k, where):
        mask = jnp.int32(0)
        for r in range(rows):
            mask = mask | (jnp.int32(1) << (col(i, r, k) & (rows - 1)))
        named, other = jnp.int32(0), jnp.int32(width)
        for r in range(rows):
            hit = (mask >> r) & 1
            place = jnp.where(hit == 1, named, other)
            rank[where * rows + r] = place
            rank[(where + 1) * rows + place] = r
            named = named + hit
            other = other + 1 - hit

    def ranked(where, r):
        return rank[where * rows + r]

    copies[0].wait()
    copies[1].wait()
    rank_rows(0, 3, 0)
    rank_rows(1, 2, 2)
    sent_1, sent_0 = jnp.where(side == ABOVE, 0, 2), jnp.where(side == ABOVE, 2, 0)
    copies[3].wait()
    for j in range(width):
        t_1[j] = t[ranked(sent_1 + 1, j)]
        t_0[j] = t[ranked(sent_0 + 1, j)]
    copies[2].wait()
    copies[4].wait()
    rank_rows(2, 2, 4)
    rank_rows(2, 3, 6)
    for j in range(width):
        note(tab, LIST_0 + j, ranked(sent_1, ranked(sent_0 + 1, j)))
        for which in (BELOW, ABOVE):
            note(tab, BACK + width * which + j, col(which, ranked(5 + 2 * which, j), 3 - which) & (rows - 1))
            for k in range(2):
                note(tab, SIDE_LAB + 8 * which + 2 * j + k, agg[col(which, ranked(5 + 2 * which, j), 2 + k)])
    for u in range(rows):
        row = ranked(sent_1 + 1, u)
        note(tab, ROW + u, row)
        note(tab, NEAR + u, ranked(sent_1, col(2, row, 1) & (rows - 1)))
        note(tab, POS2 + u, ranked(4, col(2, row, 2) & (rows - 1)))
        note(tab, POS3 + u, ranked(6, col(2, row, 3) & (rows - 1)))
        for k in range(4):
            note(tab, OWN_LAB + 4 * u + k, agg[col(2, row, k)])

    @pl.when(far_partner())
    def _():
        for copy in early:
            copy.start()
        for copy in early:
            copy.wait()
        near_blocks(tab, a, t, dinv, near_0, near_1, own, a_high, a_low, a01_high, a01_low)


def put(value, label, column):
    return jnp.where(label == column, value, jnp.zeros_like(value))


def two_columns(value, label):
    return jnp.concatenate([put(value, label, 0), put(value, label, 1)], axis=1)


def near_tiles(tab, a, t, dinv, order):
    block = t.shape[1]
    rows = [entry(tab, ROW + u) for u in order]
    prods = []
    for u, row in zip(order, rows):
        near = entry(tab, ROW + entry(tab, NEAR + u))
        prods.append(
            jnp.concatenate(
                [dot3k(*split(a[row, 0]), *split(t[row])), dot3k(*split(a[row, 1]), *split(t[near]))], axis=1
            )
        )
    tiles = []
    for u, row, prod in zip(order, rows, prods):
        smoothed = dot3k(*split(dinv[row]), *split(prod))
        p0 = t[row] - OMEGA * smoothed[:, :block]
        p1 = -OMEGA * smoothed[:, block:]
        tiles.append(two_columns(p0, entry(tab, OWN_LAB + 4 * u)) + two_columns(p1, entry(tab, OWN_LAB + 4 * u + 1)))
    return tiles


def wide(ref, *places):
    return jnp.concatenate([ref[place] for place in places], axis=0)


def near_blocks(tab, a, t, dinv, near_0, near_1, own, a_high, a_low, a01_high, a01_low):
    rows, width = own.shape[0], near_1.shape[0]
    for u, value in enumerate(near_tiles(tab, a, t, dinv, range(rows))):
        own[u] = value
        if u < width:
            near_1[u] = value
    for j in range(width):
        near_0[j] = own[entry(tab, LIST_0 + j)]
    for u in range(rows):
        row = entry(tab, ROW + u)
        a01_high[u], a01_low[u] = split(jnp.concatenate([a[row, 0], a[row, 1]], axis=1))
        for which in (BELOW, ABOVE):
            a_high[which, u], a_low[which, u] = split(a[row, 2 + which])


def near_kernel(tab, a, t, dinv, *refs):
    pl.when(jnp.logical_not(far_partner()))(lambda: near_blocks(tab, a, t, dinv, *refs[7:]))


def far_blocks(tab, a_high, a_low, dinv, t_high, t_low, order):
    prods = [
        jnp.concatenate(
            [
                dot3k(a_high[which, u], a_low[which, u], t_high[which, pos], t_low[which, pos])
                for which, pos in ((BELOW, entry(tab, POS2 + u)), (ABOVE, entry(tab, POS3 + u)))
            ],
            axis=1,
        )
        for u in order
    ]
    return [-OMEGA * dot3k(*split(dinv[entry(tab, ROW + u)]), *split(prod)) for u, prod in zip(order, prods)]


def split_rows(value, high, low):
    for j in range(value.shape[0]):
        high[j], low[j] = split(value[j])


def far_sent_kernel(tab, a_high, a_low, dinv, t_0, far_1, t_high, t_low):
    side = pair_side()
    block = dinv.shape[1]
    split_rows(t_0, t_high, t_low)
    order = range(far_1.shape[0])
    prods = []
    for u in order:
        pos = entry(tab, POS2 + 8 * side + u)
        high, low = split(dot3k(a_high[side, u], a_low[side, u], t_high[pos], t_low[pos]))
        prods.append(
            (jnp.concatenate([high, a_high[1 - side, u]], axis=1), jnp.concatenate([low, a_low[1 - side, u]], axis=1))
        )
    for u in order:
        both = -OMEGA * dot3k(*split(dinv[entry(tab, ROW + u)]), *prods[u])
        far_1[u, side] = both[:, :block]
        far_1[u, 1 - side] = both[:, block:]


def store_turned(trans, label, place, value):
    block = value.shape[0]
    trans[pl.ds(pl.multiple_of(label * block, block), block), place] = value.T
    trans[pl.ds(pl.multiple_of((1 - label) * block, block), block), place] = jnp.zeros_like(value)


def turn(tab, far, side, trans_high, trans_low):
    for u in range(far.shape[0]):
        block = far.shape[2]
        label = entry(tab, OWN_LAB + 4 * u + 2 + side)
        high, low = split(far[u, side])
        place = slice(u * block, (u + 1) * block)
        store_turned(trans_high, label, place, high)
        store_turned(trans_low, label, place, low)


def coarse_group(trans_high, trans_low, ap_high, ap_low):
    return dot3(trans_high[...], trans_low[...], ap_high[...], ap_low[...])


def far_kernel(tab, a_high, a_low, dinv, t0_high, t0_low, t_1, far_1, far_0, far, t_high, t_low):
    rows, block = far.shape[0], far.shape[2]
    width = rows // 2
    side = pair_side()
    for j in range(width):
        t_high[side, j], t_low[side, j] = t0_high[j], t0_low[j]
        t_high[1 - side, j], t_low[1 - side, j] = split(t_1[j])
    for u in range(width):
        pos = entry(tab, POS2 + 8 * (1 - side) + u)
        far[u, side] = far_1[u, side]
        far[u, 1 - side] = dot3k(*split(far_1[u, 1 - side]), t_high[1 - side, pos], t_low[1 - side, pos])
    for u, both in enumerate(far_blocks(tab, a_high, a_low, dinv, t_high, t_low, range(width, rows))):
        far[width + u, BELOW] = both[:, :block]
        far[width + u, ABOVE] = both[:, block:]
    for j in range(width):
        far_0[j] = far[entry(tab, LIST_0 + j)]


def mid_kernel(
    tab, a01_high, a01_low, a_high, a_low, far, near_0,
    trans_high, trans_low, part, ap_high, ap_low, group,
    far_high, far_low, p_high, p_low,
):
    rows, block = far.shape[0], far.shape[2]
    side = pair_side()
    split_rows(near_0, p_high, p_low)
    for u in range(rows):
        for which in (BELOW, ABOVE):
            label = entry(tab, OWN_LAB + 4 * u + 2 + which)
            high, low = split(far[u, which])
            far_high[which, u] = two_columns(high, label)
            far_low[which, u] = two_columns(low, label)

    def mine(u, which):
        near = entry(tab, NEAR + u)
        return dot3(a01_high[u], a01_low[u], wide(far_high.at[which], u, near), wide(far_low.at[which], u, near))

    totals = []
    for u in range(rows):
        pos = entry(tab, POS2 + 8 * side + u)
        totals.append(mine(u, side) + dot3k(a_high[side, u], a_low[side, u], p_high[pos], p_low[pos]))
    for u in range(rows):
        place = slice(u * block, (u + 1) * block)
        ap_high[place], ap_low[place] = split(totals[u])
    turn(tab, far, 1 - side, trans_high, trans_low)
    for u in range(rows):
        part[u] = mine(u, 1 - side)
    group[...] = coarse_group(trans_high, trans_low, ap_high, ap_low)


def first_kernel(
    tab, a_high, a_low, part, trans_high, trans_low, near_1,
    ap_high, ap_low, out_1,
    p_high, p_low,
):
    rows, block = part.shape[0], part.shape[1]
    side = 1 - pair_side()
    split_rows(near_1, p_high, p_low)
    totals = []
    for u in range(rows):
        pos = entry(tab, POS2 + 8 * side + u)
        totals.append(part[u] + dot3k(a_high[side, u], a_low[side, u], p_high[pos], p_low[pos]))
    for u in range(rows):
        place = slice(u * block, (u + 1) * block)
        ap_high[place], ap_low[place] = split(totals[u])
    out_1[...] = coarse_group(trans_high, trans_low, ap_high, ap_low)


def far_columns(tab, side, a_high, a_low, p_high, p_low, ap_high, ap_low):
    rows, block = a_high.shape[1], a_high.shape[3]
    values, here = [], []
    for u in range(rows):
        pos = entry(tab, POS2 + 8 * side + u)
        values.append(dot3k(a_high[side, u], a_low[side, u], p_high[pos], p_low[pos]))
    for u in range(rows):
        labels = SIDE_LAB + 8 * side + 2 * entry(tab, POS2 + 8 * side + u)
        here.append(two_columns(values[u][:, :block], entry(tab, labels + 1 - side)))
        high, low = split(values[u][:, block:])
        label = entry(tab, labels + side)
        place = slice(u * block, (u + 1) * block)
        ap_high[place] = two_columns(high, label)
        ap_low[place] = two_columns(low, label)
    return here


def same_kernel(
    tab, a_high, a_low, trans_high, trans_low, far_0, group,
    own_part, ap_high, ap_low, out_1,
    p_high, p_low,
):
    half = trans_high.shape[0]
    block = half // 2
    side = pair_side()
    out_1[:, :half] = group[...]
    for j in range(far_0.shape[0]):
        p_high[j, :, :block], p_low[j, :, :block] = split(far_0[j, 1 - side])
        p_high[j, :, block:], p_low[j, :, block:] = split(far_0[j, side])
    here = far_columns(tab, side, a_high, a_low, p_high, p_low, ap_high, ap_low)
    for u, value in enumerate(here):
        own_part[u] = value
    out_1[:, half:] = coarse_group(trans_high, trans_low, ap_high, ap_low)


def own_part_kernel(early, tab, a01_high, a01_low, own, t, *refs):
    own_part, back_high, back_low, own_high, own_low = refs[-5:]
    rows = own.shape[0]
    side = 1 - pair_side()

    @pl.when(far_partner() == early)
    def _():
        for j in range(rows // 2):
            back_high[j], back_low[j] = split(t[entry(tab, BACK + (rows // 2) * side + j)])
        for u in range(rows):
            own_high[u], own_low[u] = split(own[u])
        for u in range(rows):
            near = entry(tab, NEAR + u)
            own_part[u] = dot3(a01_high[u], a01_low[u], wide(own_high, u, near), wide(own_low, u, near))


def second_kernel(
    tab, a_high, a_low, own_part, so_far, back_high, back_low, trans_high, trans_low, far_1,
    own_high, own_low, ap_high, ap_low, out_1,
    p_high, p_low,
):
    rows, block = own_part.shape[0], own_part.shape[1]
    half = 2 * block
    side = 1 - pair_side()
    towards = [dot3k(*split(far_1[j, 1 - side]), back_high[j], back_low[j]) for j in range(rows // 2)]
    for j in range(rows // 2):
        p_high[j, :, :block], p_low[j, :, :block] = split(towards[j])
        p_high[j, :, block:], p_low[j, :, block:] = split(far_1[j, side])
    here = far_columns(tab, side, a_high, a_low, p_high, p_low, ap_high, ap_low)
    for u in range(rows):
        place = slice(u * block, (u + 1) * block)
        own_high[place], own_low[place] = split(own_part[u] + so_far[u] + here[u])
    out_1[:, :half] = coarse_group(trans_high, trans_low, own_high, own_low)
    out_1[:, half:] = coarse_group(trans_high, trans_low, ap_high, ap_low)


def every_group(trans_high, trans_low, aps, out):
    half = trans_high.shape[0]
    for i in range(len(aps) // 2):
        out[:, i * half : (i + 1) * half] = coarse_group(trans_high, trans_low, aps[2 * i], aps[2 * i + 1])


def other_kernel(tab, far, *refs):
    aps, (out_0, trans_high, trans_low) = refs[:10], refs[10:]
    turn(tab, far, pair_side(), trans_high, trans_low)
    every_group(trans_high, trans_low, aps, out_0)


def own_kernel(early, own, *refs):
    aps, (out, trans_high, trans_low) = refs[:10], refs[-3:]
    rows, block = own.shape[0], own.shape[1]

    @pl.when(far_partner() != early)
    def _():
        for u in range(rows):
            place = slice(u * block, (u + 1) * block)
            high, low = split(own[u])
            trans_high[:, place] = high.T
            trans_low[:, place] = low.T
        every_group(trans_high, trans_low, aps, out)


def write_slots(inverse, totals, results, out, sems):
    block = inverse.shape[1]
    inv = [split(inverse[agg]) for agg in range(2)]
    values = [dot3k(*inv[agg], *split(total)) for agg, _, total in totals]
    copies = []
    for n, ((agg, d, _), value) in enumerate(zip(totals, values)):
        results[n, 0] = value[:, :block]
        results[n, 1] = value[:, block:]
        copies.append(pltpu.make_async_copy(results.at[n], out.at[agg, pl.ds(2 * (d + 3), 2)], sems.at[n]))
        copies[-1].start()
    for copy in copies:
        copy.wait()


OWN_AT, SAME_AT = (1, -1, 2, 0, -2), (0, 2, -1, 1, 3)
PARTS_AT = (-2, -3), (-1, 1), (0,)


def finish_kernel(offsets, part_at, inverse, own, *refs):
    refs, (out, results, sems) = refs[:-3], refs[-3:]
    others = ((refs[0], SAME_AT), (refs[1], part_at)) if len(refs) > 1 else ((refs[0], part_at),)
    block = inverse.shape[1]
    half = 2 * block
    side = pair_side()

    def run(way):
        done = []
        for agg in range(2):
            line = slice(agg * block, (agg + 1) * block)
            for d in offsets:
                places = [(ref, at.index(d)) for ref, at in ((own, OWN_AT), *others) if d in at]
                shares = [ref[line, i * half : (i + 1) * half] for ref, i in places]
                done.append((agg, way * d, sum(shares[1:], shares[0])))
        write_slots(inverse, done, results, out, sems)

    pl.when(side == ABOVE)(lambda: run(1))
    pl.when(side == BELOW)(lambda: run(-1))


VMEM = pl.BlockSpec(memory_space=pltpu.VMEM)
HBM = pl.BlockSpec(memory_space=pltpu.HBM)


def call(body, outs, ins, scratch=(), micros=1.0, in_hbm=(), out_hbm=(), aliases={}):
    def specs(values, in_place):
        return [HBM if i in in_place else VMEM for i, x in enumerate(values)]

    return pl.pallas_call(
        body,
        out_shape=outs,
        in_specs=specs(ins, in_hbm),
        out_specs=specs(outs, out_hbm),
        scratch_shapes=[pltpu.VMEM(*x) if isinstance(x, tuple) else x for x in scratch],
        input_output_aliases=aliases,
        compiler_params=pltpu.CompilerParams(vmem_limit_bytes=24 * 2**20),
        cost_estimate=pl.CostEstimate(flops=int(micros * 1e9), bytes_accessed=2**20, transcendentals=0),
    )(*ins)


def shards(a, a_cols, t_blocks, t_agg, dinv, coarse_inv):
    devices = lax.axis_size(AXES)
    rows, block = t_blocks.shape[:2]
    width, half, deep = rows // 2, 2 * block, rows * block
    shape = jax.ShapeDtypeStruct
    full = lambda *dims: shape(dims, F32)
    pair = lambda *dims: [shape(dims, BF16), shape(dims, BF16)]
    two = lambda *dims: [(dims, BF16)] * 2
    tile = full(width, block, half)
    cols = a_cols.reshape(-1, ROW_CHUNK, 4).transpose(0, 2, 1).reshape(-1)

    near_shapes = [tile, tile, full(rows, block, half)] + pair(2, rows, block, block) + pair(rows, block, half)
    tab, t_0, t_1, t, *near = call(
        functools.partial(load_kernel, devices),
        [shape((TAB, LANES), jnp.int32)] + [full(width, block, block)] * 2 + [full(*t_blocks.shape)] + near_shapes,
        [pltpu.with_memory_space_constraint(x, pltpu.HBM) for x in (cols, t_agg, t_blocks, dinv, a)],
        [
            pltpu.SMEM((3 * 4 * ROW_CHUNK,), jnp.int32),
            pltpu.SMEM(t_agg.shape, jnp.int32),
            pltpu.SMEM((8 * rows,), jnp.int32),
            (dinv.shape, F32),
            (a.shape, F32),
            pltpu.SemaphoreType.DMA((7,)),
        ],
        micros=3,
        in_hbm=(0, 1, 2, 3, 4),
    )
    t_0 = exchanged(t_0, 0)
    t_1 = exchanged(t_1, 1)
    near_0, near_1, own, a23_high, a23_low, a01_high, a01_low = call(
        near_kernel, near_shapes, [tab, a, t, dinv, *near], micros=2, aliases={4 + i: i for i in range(7)}
    )
    near_0 = exchanged(near_0, 0)
    sent = full(width, 2, block, block)
    far_1, t0_high, t0_low = call(
        far_sent_kernel, [sent] + pair(width, block, block), [tab, a23_high, a23_low, dinv, t_0], micros=2
    )
    got_far_1 = exchanged(far_1, 1)

    def own_share(early, done):
        return call(
            functools.partial(own_part_kernel, early),
            [full(rows, block, half)] + pair(width, block, block),
            [tab, a01_high, a01_low, own, t, *done],
            two(rows, block, half),
            micros=1,
            aliases={5 + i: i for i in range(len(done))},
        )

    share = own_share(True, [])
    near_1 = exchanged(near_1, 1)
    far_0, far = call(
        far_kernel,
        [sent, full(rows, 2, block, block)],
        [tab, a23_high, a23_low, dinv, t0_high, t0_low, t_1, far_1],
        two(2, width, block, block),
        micros=1,
    )
    far_0, far_1 = exchanged(far_0, 0), got_far_1
    out_high, out_low, part, ap_e1_high, ap_e1_low, group = call(
        mid_kernel,
        pair(half, deep) + [full(rows, block, half)] + pair(deep, half) + [full(half, half)],
        [tab, a01_high, a01_low, a23_high, a23_low, far, near_0],
        two(2, rows, block, half) + two(width, block, half),
        micros=2,
    )
    part_own, ap_e2_high, ap_e2_low, part_1 = call(
        same_kernel,
        [full(rows, block, half)] + pair(deep, half) + [full(half, 2 * half)],
        [tab, a23_high, a23_low, out_high, out_low, far_0, group],
        two(width, block, half),
        micros=1,
    )
    part_1 = exchanged(part_1, 1)
    share_own, back_high, back_low = own_share(False, share)
    ap_own_high, ap_own_low, ap_o2_high, ap_o2_low, part_2 = call(
        second_kernel,
        pair(deep, half) * 2 + [full(half, 2 * half)],
        [tab, a23_high, a23_low, share_own, part_own, back_high, back_low, out_high, out_low, far_1],
        two(width, block, half),
        micros=2,
    )
    part_2 = exchanged(part_2, 1)
    ap_o1_high, ap_o1_low, part_3 = call(
        first_kernel,
        pair(deep, half) + [full(half, half)],
        [tab, a23_high, a23_low, part, out_high, out_low, near_1],
        two(width, block, half),
        micros=2,
    )
    part_3 = exchanged(part_3, 1)
    aps = [
        ap_e1_high, ap_e1_low, ap_o1_high, ap_o1_low, ap_e2_high, ap_e2_low,
        ap_own_high, ap_own_low, ap_o2_high, ap_o2_low,
    ]
    (both_0,) = call(other_kernel, [full(half, 5 * half)], [tab, far] + aps, two(half, deep), micros=2)
    total = []
    for early in (True, False):
        total = call(
            functools.partial(own_kernel, early),
            [full(half, 5 * half)],
            [own] + aps + total,
            two(half, deep),
            micros=2,
            aliases={11: 0} if total else {},
        )
        total = list(total)
        if early:
            both_0 = exchanged(both_0, 0)
    (total,) = total
    out = []
    for i, (offsets, got) in enumerate((((-3, -2), part_1), ((-1, 1, 2, 3), part_2), ((0,), part_3))):
        n = 2 * len(offsets)
        out = call(
            functools.partial(finish_kernel, offsets, PARTS_AT[i]),
            [full(2, 14, block, block)],
            [coarse_inv, total] + ([both_0] if i else []) + [got, *out],
            [((n, 2, block, block), F32), pltpu.SemaphoreType.DMA((n,))],
            micros=1,
            in_hbm=(4,),
            out_hbm=(0,),
            aliases={4: 0} if i else {},
        )
    return out[0]


def solution(mesh):
    placed = (
        P(AXES, None, None, None),
        P(),
        P(AXES, None, None),
        P(),
        P(AXES, None, None),
        P(AXES, None, None),
    )
    return jax.shard_map(
        shards,
        mesh=mesh,
        in_specs=placed,
        out_specs=P(AXES, None, None, None),
        check_vma=False,
    )
```

profile of v0, /device:TPU:0, one launch (start us, length us, event | category | flops | bytes accessed | tf_op | source)
XLA Modules:
  0.0 59.7 jit_solution(11444138213062317437)
XLA Ops:
  0.0 4.5 %shard_map.64 = (s32[96,128]{1,0:T(8,128)S(1)}, f32[4,128,128]{2,1,0:T(8,128)S(1)}, f32[4,128,128]{2,1,0:T(8,128)S(1)}, f32[8,128,128]{2,1,0:T(8,128)S(1)}, f32[...) custom-call(s32[4096]{0:T(1024)} %bitcast.5, ...), custom_call_target="tpu_custom_call" | custom-call | flops 3000000000 | bytes 1048576 | tf_op jit(solution)/shard_map/pallas_call | solution.py:470
  4.5 0.1 collective-permute-start
  4.6 5.9 %collective-permute-start.1 = (f32[4,128,128]{2,1,0:T(8,128)S(1)}, f32[4,128,128]{2,1,0:T(8,128)S(1)}, u32[]{:S(2)}, u32[]{:S(2)}) collective-permute-start(f32[4,128,128]{2,1,0:T(8,128)S(1)} %get-tuple-element.69), channel_id=1, source_target_pairs={{1,2},{2,1},{3,4},{4,3},{5,6},{6,5},{7,8},{8,7},{9,10},{10,9},{11,... | collective-permute-start | bytes 786440 | tf_op jit(solution)/shard_map/ppermute | solution.py:27
  10.5 0.0 collective-permute-start.2
  10.5 2.8 %collective-permute-start.3 = (f32[4,128,256]{2,1,0:T(8,128)S(1)}, f32[4,128,256]{2,1,0:T(8,128)S(1)}, u32[]{:S(2)}, u32[]{:S(2)}) collective-permute-start(f32[4,128,256]{2,1,0:T(8,128)S(1)} %get-tuple-element.78), channel_id=1, source_target_pairs={{1,2},{2,1},{3,4},{4,3},{5,6},{6,5},{7,8},{8,7},{9,10},{10,9},{11,... | collective-permute-start | bytes 1572872 | tf_op jit(solution)/shard_map/ppermute | solution.py:27
  13.3 0.0 collective-permute-done.t_0
  13.3 0.5 shard_map.66
  13.9 2.1 %collective-permute-done.1.t_1 = f32[4,128,128]{2,1,0:T(8,128)S(1)} collective-permute-done((f32[4,128,128]{2,1,0:T(8,128)S(1)}, f32[4,128,128]{2,1,0:T(8,128)S(1)}, u32[]{:S(2)}, u32[]{:S(2)}) %collective-permute-start.1) | collective-permute-done | bytes 262176 | tf_op jit(solution)/shard_map/ppermute | solution.py:27
  15.9 0.8 %shard_map.67 = (f32[4,2,128,128]{3,2,1,0:T(8,128)S(1)}, f32[8,2,128,128]{3,2,1,0:T(8,128)S(1)}) custom-call(s32[96,128]{1,0:T(8,128)S(1)} %get-tuple-element.52.tab, bf16[2,8,128,128]{3,2,1,0:T(8,128)(2,1)S(1)} %get-tuple-element.64.a_high, bf16[2,8,128,128]{3,2,1,0:T(8,128)(2,1)S(1)} %get-tuple-element.65.a_low, f32[8,128,128]{2,1,0:T(8,128)S(1)} %copy-done.2, ...), custom_call_target="tpu_custom_call" | custom-call | flops 1000000000 | bytes 1048576 | tf_op jit(solution)/shard_map/pallas_call | solution.py:470
  16.7 0.1 collective-permute-start.4
  16.8 0.8 %shard_map.71 = (f32[8,128,256]{2,1,0:T(8,128)S(1)}, bf16[4,128,128]{2,1,0:T(8,128)(2,1)S(1)}, bf16[4,128,128]{2,1,0:T(8,128)(2,1)S(1)}) custom-call(s32[96,128]{1,0:T(8,128)S(1)} %get-tuple-element.52.tab, bf16[8,128,256]{2,1,0:T(8,128)(2,1)S(1)} %get-tuple-element.62.a01_high, bf16[8,128,256]{2,1,0:T(8,128)(2,1)S(1)} %get-tuple-element.63.a01_low, ...), custom_call_target="tpu_custom_call" | custom-call | flops 1000000000 | bytes 1048576 | tf_op jit(solution)/shard_map/pallas_call | solution.py:470
  17.6 5.1 %collective-permute-start.5 = (f32[4,2,128,128]{3,2,1,0:T(8,128)S(1)}, f32[4,2,128,128]{3,2,1,0:T(8,128)S(1)}, u32[]{:S(2)}, u32[]{:S(2)}) collective-permute-start(f32[4,2,128,128]{3,2,1,0:T(8,128)S(1)} %get-tuple-element.70.far_1), channel_id=1, source_target_pairs={{1,2},{2,1},{3,4},{4,3},{5,6},{6,5},{7,8},{8,7},{9,10},{10,9},{11,... | collective-permute-start | bytes 1572872 | tf_op jit(solution)/shard_map/ppermute | solution.py:27
  22.7 0.0 collective-permute-done.2.near_0
  22.7 2.2 %shard_map.68 = (bf16[256,1024]{1,0:T(8,128)(2,1)S(1)}, bf16[256,1024]{1,0:T(8,128)(2,1)S(1)}, f32[8,128,256]{2,1,0:T(8,128)S(1)}, bf16[1024,256]{1,0:T(8,128)(2...) custom-call(s32[96,128]{1,0:T(8,128)S(1)} %get-tuple-element.52.tab, ...), custom_call_target="tpu_custom_call" | custom-call | flops 2000000000 | bytes 1048576 | tf_op jit(solution)/shard_map/pallas_call | solution.py:470
  24.9 0.0 collective-permute-done.3.near_1
  24.9 1.0 %shard_map.69 = (bf16[1024,256]{1,0:T(8,128)(2,1)S(1)}, bf16[1024,256]{1,0:T(8,128)(2,1)S(1)}, f32[256,256]{1,0:T(8,128)S(1)}) custom-call(s32[96,128]{1,0:T(8,128)S(1)} %get-tuple-element.52.tab, bf16[2,8,128,128]{3,2,1,0:T(8,128)(2,1)S(1)} %get-tuple-element.64.a_high, bf16[2,8,128,128]{3,2,1,0:T(8,128)(2,1)S(1)} %get-tuple-element.65.a_low, ...), custom_call_target="tpu_custom_call" | custom-call | flops 2000000000 | bytes 1048576 | tf_op jit(solution)/shard_map/pallas_call | solution.py:470
  25.9 1.1 %shard_map.70 = (f32[8,128,256]{2,1,0:T(8,128)S(1)}, bf16[1024,256]{1,0:T(8,128)(2,1)S(1)}, bf16[1024,256]{1,0:T(8,128)(2,1)S(1)}, f32[256,512]{1,0:T(8,128)S(1)}) custom-call(s32[96,128]{1,0:T(8,128)S(1)} %get-tuple-element.52.tab, bf16[2,8,128,128]{3,2,1,0:T(8,128)(2,1)S(1)} %get-tuple-element.64.a_high, ...), custom_call_target="tpu_custom_call" | custom-call | flops 1000000000 | bytes 1048576 | tf_op jit(solution)/shard_map/pallas_call | solution.py:470
  27.0 4.7 %collective-permute-done.5.far_1 = f32[4,2,128,128]{3,2,1,0:T(8,128)S(1)} collective-permute-done((f32[4,2,128,128]{3,2,1,0:T(8,128)S(1)}, f32[4,2,128,128]{3,2,1,0:T(8,128)S(1)}, u32[]{:S(2)}, u32[]{:S(2)}) %collective-permute-start.5) | collective-permute-done | bytes 524320 | tf_op jit(solution)/shard_map/ppermute | solution.py:27
  31.7 1.7 %shard_map.73 = (bf16[1024,256]{1,0:T(8,128)(2,1)S(1)}, bf16[1024,256]{1,0:T(8,128)(2,1)S(1)}, bf16[1024,256]{1,0:T(8,128)(2,1)S(1)}, bf16[1024,256]{1,0:T(8,128)(2,1)S(1)}, f32[256,512]{1,0:T(8,128)S(1)}) custom-call(s32[96,128]{1,0:T(8,128)S(1)} %get-tuple-element.52.tab, bf16[2,8,128,128]{3,2,1,0:T(8,128)(2,1)S(1)} %get-tuple-element.64.a_high, ...), custom_call_target="tpu_custom_call" | custom-call | flops 2000000000 | bytes 1048576 | tf_op jit(solution)/shard_map/pallas_call | solution.py:470
  33.4 2.5 %shard_map.76 = f32[256,1280]{1,0:T(8,128)S(1)} custom-call(s32[96,128]{1,0:T(8,128)S(1)} %get-tuple-element.52.tab, f32[8,2,128,128]{3,2,1,0:T(8,128)S(1)} %get-tuple-element.71.far, bf16[1024,256]{1,0:T(8,128)(2,1)S(1)} %get-tuple-element.73.refs_0_, bf16[1024,256]{1,0:T(8,128)(2,1)S(1)} %get-tuple-element.74.refs_1_, ...), custom_call_target="tpu_custom_call" | custom-call | flops 2000000000 | bytes 1048576 | tf_op jit(solution)/shard_map/pallas_call | solution.py:470
  35.9 0.1 collective-permute-start.6
  36.0 5.1 %collective-permute-start.9 = (f32[256,512]{1,0:T(8,128)S(1)}, f32[256,512]{1,0:T(8,128)S(1)}, u32[]{:S(2)}, u32[]{:S(2)}) collective-permute-start(f32[256,512]{1,0:T(8,128)S(1)} %get-tuple-element.98), channel_id=1, source_target_pairs={{1,2},{2,1},{3,4},{4,3},{5,6},{6,5},{7,8},{8,7},{9,10},{10,9},{11,... | collective-permute-start | bytes 1572872 | tf_op jit(solution)/shard_map/ppermute | solution.py:27
  41.1 2.1 %collective-permute-start.8 = (f32[256,512]{1,0:T(8,128)S(1)}, f32[256,512]{1,0:T(8,128)S(1)}, u32[]{:S(2)}, u32[]{:S(2)}) collective-permute-start(f32[256,512]{1,0:T(8,128)S(1)} %get-tuple-element.97), channel_id=1, source_target_pairs={{1,2},{2,1},{3,4},{4,3},{5,6},{6,5},{7,8},{8,7},{9,10},{10,9},{11,... | collective-permute-start | bytes 1572872 | tf_op jit(solution)/shard_map/ppermute | solution.py:27
  43.2 5.1 %collective-permute-start.7 = (f32[256,256]{1,0:T(8,128)S(1)}, f32[256,256]{1,0:T(8,128)S(1)}, u32[]{:S(2)}, u32[]{:S(2)}) collective-permute-start(f32[256,256]{1,0:T(8,128)S(1)} %get-tuple-element.96), channel_id=1, source_target_pairs={{1,2},{2,1},{3,4},{4,3},{5,6},{6,5},{7,8},{8,7},{9,10},{10,9},{11,... | collective-permute-start | bytes 786440 | tf_op jit(solution)/shard_map/ppermute | solution.py:27
  48.3 2.3 %shard_map.75.own = f32[256,1280]{1,0:T(8,128)S(1)} custom-call(f32[8,128,256]{2,1,0:T(8,128)S(1)} %get-tuple-element.61.own, bf16[1024,256]{1,0:T(8,128)(2,1)S(1)} %get-tuple-element.73.refs_0_, bf16[1024,256]{1,0:T(8,128)(2,1)S(1)} %get-tuple-element.74.refs_1_, bf16[1024,256]{1,0:T(8,128)(2,1)S(1)} %get-tuple-element.79.refs_2_, ...), custom_call_target="tpu_custom_call", output_to_operand_aliasing={{}: (11, {})} | custom-call | flops 2000000000 | bytes 1048576 | tf_op jit(solution)/shard_map/pallas_call | solution.py:470
  50.6 0.0 collective-permute-done.9.refs_0_
  50.6 1.1 %shard_map.77.refs_2_ = f32[2,14,128,128]{3,2,1,0:T(8,128)} custom-call(f32[2,128,128]{2,1,0:T(8,128)S(1)} %copy-done, f32[256,1280]{1,0:T(8,128)S(1)} %shard_map.75.own, f32[256,512]{1,0:T(8,128)S(1)} %collective-permute-done.9.refs_0_), custom_call_target="tpu_custom_call" | custom-call | flops 1000000000 | bytes 1048576 | tf_op jit(solution)/shard_map/pallas_call | solution.py:470
  51.7 4.0 %collective-permute-done.8.refs_1_ = f32[256,512]{1,0:T(8,128)S(1)} collective-permute-done((f32[256,512]{1,0:T(8,128)S(1)}, f32[256,512]{1,0:T(8,128)S(1)}, u32[]{:S(2)}, u32[]{:S(2)}) %collective-permute-start.8) | collective-permute-done | bytes 524320 | tf_op jit(solution)/shard_map/ppermute | solution.py:27
  55.7 0.0 collective-permute-done.6.refs_0_
  55.7 1.3 %shard_map.78.refs_2_ = f32[2,14,128,128]{3,2,1,0:T(8,128)} custom-call(f32[2,128,128]{2,1,0:T(8,128)S(1)} %copy-done, f32[256,1280]{1,0:T(8,128)S(1)} %shard_map.75.own, f32[256,1280]{1,0:T(8,128)S(1)} %collective-permute-done.6.refs_0_, f32[256,512]{1,0:T(8,128)S(1)} %collective-permute-done.8.refs_1_, ...), custom_call_target="tpu_custom_call", output_to_operand_aliasing={{}: (4, {})} | custom-call | flops 1000000000 | bytes 1048576 | tf_op jit(solution)/shard_map/pallas_call | solution.py:470
  57.0 1.5 %collective-permute-done.7.refs_1_ = f32[256,256]{1,0:T(8,128)S(1)} collective-permute-done((f32[256,256]{1,0:T(8,128)S(1)}, f32[256,256]{1,0:T(8,128)S(1)}, u32[]{:S(2)}, u32[]{:S(2)}) %collective-permute-start.7) | collective-permute-done | bytes 262176 | tf_op jit(solution)/shard_map/ppermute | solution.py:27
  58.5 1.0 %shard_map.79 = f32[2,14,128,128]{3,2,1,0:T(8,128)} custom-call(f32[2,128,128]{2,1,0:T(8,128)S(1)} %copy-done, f32[256,1280]{1,0:T(8,128)S(1)} %shard_map.75.own, f32[256,1280]{1,0:T(8,128)S(1)} %collective-permute-done.6.refs_0_, f32[256,256]{1,0:T(8,128)S(1)} %collective-permute-done.7.refs_1_, ...), custom_call_target="tpu_custom_call", output_to_operand_aliasing={{}: (4, {})} | custom-call | flops 1000000000 | bytes 1048576 | tf_op jit(solution)/shard_map/pallas_call | solution.py:470
  (10 shorter events, 0.0 us)
Async XLA Ops:
  0.0 10.5 %copy-start.1 = (f32[8,4,128,128]{3,2,1,0:T(8,128)S(1)}, f32[8,4,128,128]{3,2,1,0:T(8,128)}, u32[]{:S(2)}) copy-start(f32[8,4,128,128]{3,2,1,0:T(8,128)} %a.1) | copy-start | bytes 6291460
  0.0 10.5 %copy-start.2 = (f32[8,128,128]{2,1,0:T(8,128)S(1)}, f32[8,128,128]{2,1,0:T(8,128)}, u32[]{:S(2)}) copy-start(f32[8,128,128]{2,1,0:T(8,128)} %dinv.5) | copy-start | bytes 1572868
  4.5 8.8 %collective-permute-start = (f32[4,128,128]{2,1,0:T(8,128)S(1)}, f32[4,128,128]{2,1,0:T(8,128)S(1)}, u32[]{:S(2)}, u32[]{:S(2)}) collective-permute-start(f32[4,128,128]{2,1,0:T(8,128)S(1)} %get-tuple-element.66), channel_id=1, source_target_pairs={{0,1},{1,0},{2,3},{3,2},{4,5},{5,4},{6,7},{7,6},{8,9},{9,8},{10,11... | collective-permute-start | bytes 786440 | tf_op jit(solution)/shard_map/ppermute | solution.py:27
  4.6 11.3 %collective-permute-start.1 = (f32[4,128,128]{2,1,0:T(8,128)S(1)}, f32[4,128,128]{2,1,0:T(8,128)S(1)}, u32[]{:S(2)}, u32[]{:S(2)}) collective-permute-start(f32[4,128,128]{2,1,0:T(8,128)S(1)} %get-tuple-element.69), channel_id=1, source_target_pairs={{1,2},{2,1},{3,4},{4,3},{5,6},{6,5},{7,8},{8,7},{9,10},{10,9},{11,... | collective-permute-start | bytes 786440 | tf_op jit(solution)/shard_map/ppermute | solution.py:27
  10.5 12.2 %collective-permute-start.2 = (f32[4,128,256]{2,1,0:T(8,128)S(1)}, f32[4,128,256]{2,1,0:T(8,128)S(1)}, u32[]{:S(2)}, u32[]{:S(2)}) collective-permute-start(f32[4,128,256]{2,1,0:T(8,128)S(1)} %get-tuple-element.72), channel_id=1, source_target_pairs={{0,1},{1,0},{2,3},{3,2},{4,5},{5,4},{6,7},{7,6},{8,9},{9,8},{10,11... | collective-permute-start | bytes 1572872 | tf_op jit(solution)/shard_map/ppermute | solution.py:27
  10.5 14.4 %collective-permute-start.3 = (f32[4,128,256]{2,1,0:T(8,128)S(1)}, f32[4,128,256]{2,1,0:T(8,128)S(1)}, u32[]{:S(2)}, u32[]{:S(2)}) collective-permute-start(f32[4,128,256]{2,1,0:T(8,128)S(1)} %get-tuple-element.78), channel_id=1, source_target_pairs={{1,2},{2,1},{3,4},{4,3},{5,6},{6,5},{7,8},{8,7},{9,10},{10,9},{11,... | collective-permute-start | bytes 1572872 | tf_op jit(solution)/shard_map/ppermute | solution.py:27
  16.7 9.2 %collective-permute-start.4 = (f32[4,2,128,128]{3,2,1,0:T(8,128)S(1)}, f32[4,2,128,128]{3,2,1,0:T(8,128)S(1)}, u32[]{:S(2)}, u32[]{:S(2)}) collective-permute-start(f32[4,2,128,128]{3,2,1,0:T(8,128)S(1)} %get-tuple-element.81), channel_id=1, source_target_pairs={{0,1},{1,0},{2,3},{3,2},{4,5},{5,4},{6,7},{7,6},{8,9},{9,8},{10,11... | collective-permute-start | bytes 1572872 | tf_op jit(solution)/shard_map/ppermute | solution.py:27
  17.6 14.1 %collective-permute-start.5 = (f32[4,2,128,128]{3,2,1,0:T(8,128)S(1)}, f32[4,2,128,128]{3,2,1,0:T(8,128)S(1)}, u32[]{:S(2)}, u32[]{:S(2)}) collective-permute-start(f32[4,2,128,128]{3,2,1,0:T(8,128)S(1)} %get-tuple-element.70.far_1), channel_id=1, source_target_pairs={{1,2},{2,1},{3,4},{4,3},{5,6},{6,5},{7,8},{8,7},{9,10},{10,9},{11,... | collective-permute-start | bytes 1572872 | tf_op jit(solution)/shard_map/ppermute | solution.py:27
  35.9 19.8 %collective-permute-start.6 = (f32[256,1280]{1,0:T(8,128)S(1)}, f32[256,1280]{1,0:T(8,128)S(1)}, u32[]{:S(2)}, u32[]{:S(2)}) collective-permute-start(f32[256,1280]{1,0:T(8,128)S(1)} %shard_map.76), channel_id=1, source_target_pairs={{0,1},{1,0},{2,3},{3,2},{4,5},{5,4},{6,7},{7,6},{8,9},{9,8},{10,11... | collective-permute-start | bytes 3932168 | tf_op jit(solution)/shard_map/ppermute | solution.py:27
  36.0 14.6 %collective-permute-start.9 = (f32[256,512]{1,0:T(8,128)S(1)}, f32[256,512]{1,0:T(8,128)S(1)}, u32[]{:S(2)}, u32[]{:S(2)}) collective-permute-start(f32[256,512]{1,0:T(8,128)S(1)} %get-tuple-element.98), channel_id=1, source_target_pairs={{1,2},{2,1},{3,4},{4,3},{5,6},{6,5},{7,8},{8,7},{9,10},{10,9},{11,... | collective-permute-start | bytes 1572872 | tf_op jit(solution)/shard_map/ppermute | solution.py:27
  41.1 14.6 %collective-permute-start.8 = (f32[256,512]{1,0:T(8,128)S(1)}, f32[256,512]{1,0:T(8,128)S(1)}, u32[]{:S(2)}, u32[]{:S(2)}) collective-permute-start(f32[256,512]{1,0:T(8,128)S(1)} %get-tuple-element.97), channel_id=1, source_target_pairs={{1,2},{2,1},{3,4},{4,3},{5,6},{6,5},{7,8},{8,7},{9,10},{10,9},{11,... | collective-permute-start | bytes 1572872 | tf_op jit(solution)/shard_map/ppermute | solution.py:27
  43.2 15.3 %collective-permute-start.7 = (f32[256,256]{1,0:T(8,128)S(1)}, f32[256,256]{1,0:T(8,128)S(1)}, u32[]{:S(2)}, u32[]{:S(2)}) collective-permute-start(f32[256,256]{1,0:T(8,128)S(1)} %get-tuple-element.96), channel_id=1, source_target_pairs={{1,2},{2,1},{3,4},{4,3},{5,6},{6,5},{7,8},{8,7},{9,10},{10,9},{11,... | collective-permute-start | bytes 786440 | tf_op jit(solution)/shard_map/ppermute | solution.py:27
  48.3 2.3 %copy-start = (f32[2,128,128]{2,1,0:T(8,128)S(1)}, f32[2,128,128]{2,1,0:T(8,128)}, u32[]{:S(2)}) copy-start(f32[2,128,128]{2,1,0:T(8,128)} %inverse.5) | copy-start | bytes 393220
where the time goes:
time: 59.8 us; the launch traced here: 59.7 us
  starting transfers between devices  26.4 us (44%)
  Pallas kernels  20.6 us (34%)
  waiting for transfers between devices  12.3 us (21%)
    ppermute x10, starting transfers between devices, exchanged(): return lax.ppermute(value, AXES, pairs)  26.4 us
    pallas_call x16, Pallas kernels, call(): pl.pallas_call(body, out_shape=outs, in_specs=specs(ins, in_hbm), out_spe...  20.6 us
    ppermute x10, waiting for transfers between devices, exchanged(): return lax.ppermute(value, AXES, pairs)  12.3 us
  transfers between devices with their start and end apart: 10, of which 4 were waited for; matrix products, arithmetic and copies ran while one was open for 0% of the time, Pallas kernels for 18%

commit v1 on v0

--- a/solution.py
+++ b/solution.py
@@ -79,20 +79,36 @@
     side = pair_side()
     shift = ROW_CHUNK.bit_length() - 1
     chunk = 4 * ROW_CHUNK
+    at_1 = [(slab * rows) >> shift for slab in slabs[:2]]
+    at_2 = [(lax.rem(device + step, devices) * rows) >> shift for step in (devices - 2, 2)]
     copies = [
         pltpu.make_async_copy(
-            cols_hbm.at[pl.ds(pl.multiple_of(((slab * rows) >> shift) * chunk, chunk), chunk)],
-            cols.at[pl.ds(i * chunk, chunk)],
-            sem.at[i],
-        )
-        for i, slab in enumerate(slabs)
+            cols_hbm.at[pl.ds(pl.multiple_of(at_1[i] * chunk, chunk), chunk)], cols.at[pl.ds(i * chunk, chunk)], sem.at[i]
+        )
+        for i in range(2)
     ]
-    copies += [pltpu.make_async_copy(t_hbm, t, sem.at[3]), pltpu.make_async_copy(agg_hbm, agg, sem.at[4])]
-    for i, copy in enumerate(copies):
-        copy.start(priority=1 if i == 3 else 0)
+    copies += [pltpu.make_async_copy(t_hbm, t, sem.at[2])]
+    copies += [
+        pltpu.make_async_copy(
+            agg_hbm.at[pl.ds(pl.multiple_of(at_2[i] * ROW_CHUNK, ROW_CHUNK), ROW_CHUNK)],
+            agg.at[pl.ds(i * ROW_CHUNK, ROW_CHUNK)],
+            sem.at[3 + i],
+        )
+        for i in range(2)
+    ]
+    for copy in copies:
+        copy.start()
+    own_at = jnp.where((device * rows) >> shift == at_1[0], 0, 1)
+    starts = [
+        held * chunk + ((slab * rows) & (ROW_CHUNK - 1)) for held, slab in zip((0, 1, own_at), slabs)
+    ]
 
     def col(i, r, k):
-        return cols[i * chunk + k * ROW_CHUNK + ((slabs[i] * rows) & (ROW_CHUNK - 1)) + r]
+        return cols[starts[i] + k * ROW_CHUNK + r]
+
+    def label_of(row):
+        held = jnp.where(row >> shift == at_2[0], 0, ROW_CHUNK)
+        return agg[held + (row & (ROW_CHUNK - 1))]
 
     def rank_rows(i, k, where):
         mask = jnp.int32(0)
@@ -115,11 +131,11 @@
     rank_rows(0, 3, 0)
     rank_rows(1, 2, 2)
     sent_1, sent_0 = jnp.where(side == ABOVE, 0, 2), jnp.where(side == ABOVE, 2, 0)
-    copies[3].wait()
+    copies[2].wait()
     for j in range(width):
         t_1[j] = t[ranked(sent_1 + 1, j)]
         t_0[j] = t[ranked(sent_0 + 1, j)]
-    copies[2].wait()
+    copies[3].wait()
     copies[4].wait()
     rank_rows(2, 2, 4)
     rank_rows(2, 3, 6)
@@ -128,7 +144,7 @@
         for which in (BELOW, ABOVE):
             note(tab, BACK + width * which + j, col(which, ranked(5 + 2 * which, j), 3 - which) & (rows - 1))
             for k in range(2):
-                note(tab, SIDE_LAB + 8 * which + 2 * j + k, agg[col(which, ranked(5 + 2 * which, j), 2 + k)])
+                note(tab, SIDE_LAB + 8 * which + 2 * j + k, label_of(col(which, ranked(5 + 2 * which, j), 2 + k)))
     for u in range(rows):
         row = ranked(sent_1 + 1, u)
         note(tab, ROW + u, row)
@@ -136,7 +152,7 @@
         note(tab, POS2 + u, ranked(4, col(2, row, 2) & (rows - 1)))
         note(tab, POS3 + u, ranked(6, col(2, row, 3) & (rows - 1)))
         for k in range(4):
-            note(tab, OWN_LAB + 4 * u + k, agg[col(2, row, k)])
+            note(tab, OWN_LAB + 4 * u + k, label_of(col(2, row, k)))
 
     @pl.when(far_partner())
     def _():
@@ -496,8 +512,8 @@
         [shape((TAB, LANES), jnp.int32)] + [full(width, block, block)] * 2 + [full(*t_blocks.shape)] + near_shapes,
         [pltpu.with_memory_space_constraint(x, pltpu.HBM) for x in (cols, t_agg, t_blocks, dinv, a)],
         [
-            pltpu.SMEM((3 * 4 * ROW_CHUNK,), jnp.int32),
-            pltpu.SMEM(t_agg.shape, jnp.int32),
+            pltpu.SMEM((2 * 4 * ROW_CHUNK,), jnp.int32),
+            pltpu.SMEM((2 * ROW_CHUNK,), jnp.int32),
             pltpu.SMEM((8 * rows,), jnp.int32),
             (dinv.shape, F32),
             (a.shape, F32),

time: 59.8 us -> 59.9 us (level)
  no operation moved by 1% of the time
where the time goes in v1:
time: 59.9 us; the launch traced here: 59.7 us
  starting transfers between devices  26.4 us (44%)
  Pallas kernels  20.7 us (35%)
  waiting for transfers between devices  12.3 us (21%)
    ppermute x10, starting transfers between devices, exchanged(): return lax.ppermute(value, AXES, pairs)  26.4 us
    pallas_call x16, Pallas kernels, call(): pl.pallas_call(body, out_shape=outs, in_specs=specs(ins, in_hbm), out_spe...  20.7 us
    ppermute x10, waiting for transfers between devices, exchanged(): return lax.ppermute(value, AXES, pairs)  12.3 us
  transfers between devices with their start and end apart: 10, of which 4 were waited for; matrix products, arithmetic and copies ran while one was open for 0% of the time, Pallas kernels for 18%

profile of v1, /device:TPU:0, one launch (start us, length us, event | category | flops | bytes accessed | tf_op | source)
XLA Modules:
  0.0 59.7 jit_solution(9268292827954966331)
XLA Ops:
  0.0 4.6 %shard_map.64 = (s32[96,128]{1,0:T(8,128)S(1)}, f32[4,128,128]{2,1,0:T(8,128)S(1)}, f32[4,128,128]{2,1,0:T(8,128)S(1)}, f32[8,128,128]{2,1,0:T(8,128)S(1)}, f32[...) custom-call(s32[4096]{0:T(1024)} %bitcast.5, ...), custom_call_target="tpu_custom_call" | custom-call | flops 3000000000 | bytes 1048576 | tf_op jit(solution)/shard_map/pallas_call | solution.py:486
  4.6 0.1 collective-permute-start
  4.7 5.9 %collective-permute-start.1 = (f32[4,128,128]{2,1,0:T(8,128)S(1)}, f32[4,128,128]{2,1,0:T(8,128)S(1)}, u32[]{:S(2)}, u32[]{:S(2)}) collective-permute-start(f32[4,128,128]{2,1,0:T(8,128)S(1)} %get-tuple-element.69), channel_id=1, source_target_pairs={{1,2},{2,1},{3,4},{4,3},{5,6},{6,5},{7,8},{8,7},{9,10},{10,9},{11,... | collective-permute-start | bytes 786440 | tf_op jit(solution)/shard_map/ppermute | solution.py:27
  10.6 0.0 collective-permute-start.2
  10.6 2.8 %collective-permute-start.3 = (f32[4,128,256]{2,1,0:T(8,128)S(1)}, f32[4,128,256]{2,1,0:T(8,128)S(1)}, u32[]{:S(2)}, u32[]{:S(2)}) collective-permute-start(f32[4,128,256]{2,1,0:T(8,128)S(1)} %get-tuple-element.78), channel_id=1, source_target_pairs={{1,2},{2,1},{3,4},{4,3},{5,6},{6,5},{7,8},{8,7},{9,10},{10,9},{11,... | collective-permute-start | bytes 1572872 | tf_op jit(solution)/shard_map/ppermute | solution.py:27
  13.4 0.0 collective-permute-done.t_0
  13.4 0.5 shard_map.66
  13.9 2.1 %collective-permute-done.1.t_1 = f32[4,128,128]{2,1,0:T(8,128)S(1)} collective-permute-done((f32[4,128,128]{2,1,0:T(8,128)S(1)}, f32[4,128,128]{2,1,0:T(8,128)S(1)}, u32[]{:S(2)}, u32[]{:S(2)}) %collective-permute-start.1) | collective-permute-done | bytes 262176 | tf_op jit(solution)/shard_map/ppermute | solution.py:27
  16.0 0.8 %shard_map.67 = (f32[4,2,128,128]{3,2,1,0:T(8,128)S(1)}, f32[8,2,128,128]{3,2,1,0:T(8,128)S(1)}) custom-call(s32[96,128]{1,0:T(8,128)S(1)} %get-tuple-element.52.tab, bf16[2,8,128,128]{3,2,1,0:T(8,128)(2,1)S(1)} %get-tuple-element.64.a_high, bf16[2,8,128,128]{3,2,1,0:T(8,128)(2,1)S(1)} %get-tuple-element.65.a_low, f32[8,128,128]{2,1,0:T(8,128)S(1)} %copy-done.2, ...), custom_call_target="tpu_custom_call" | custom-call | flops 1000000000 | bytes 1048576 | tf_op jit(solution)/shard_map/pallas_call | solution.py:486
  16.8 0.1 collective-permute-start.4
  16.9 0.8 %shard_map.71 = (f32[8,128,256]{2,1,0:T(8,128)S(1)}, bf16[4,128,128]{2,1,0:T(8,128)(2,1)S(1)}, bf16[4,128,128]{2,1,0:T(8,128)(2,1)S(1)}) custom-call(s32[96,128]{1,0:T(8,128)S(1)} %get-tuple-element.52.tab, bf16[8,128,256]{2,1,0:T(8,128)(2,1)S(1)} %get-tuple-element.62.a01_high, bf16[8,128,256]{2,1,0:T(8,128)(2,1)S(1)} %get-tuple-element.63.a01_low, ...), custom_call_target="tpu_custom_call" | custom-call | flops 1000000000 | bytes 1048576 | tf_op jit(solution)/shard_map/pallas_call | solution.py:486
  17.6 5.1 %collective-permute-start.5 = (f32[4,2,128,128]{3,2,1,0:T(8,128)S(1)}, f32[4,2,128,128]{3,2,1,0:T(8,128)S(1)}, u32[]{:S(2)}, u32[]{:S(2)}) collective-permute-start(f32[4,2,128,128]{3,2,1,0:T(8,128)S(1)} %get-tuple-element.70.far_1), channel_id=1, source_target_pairs={{1,2},{2,1},{3,4},{4,3},{5,6},{6,5},{7,8},{8,7},{9,10},{10,9},{11,... | collective-permute-start | bytes 1572872 | tf_op jit(solution)/shard_map/ppermute | solution.py:27
  22.8 0.0 collective-permute-done.2.near_0
  22.8 2.2 %shard_map.68 = (bf16[256,1024]{1,0:T(8,128)(2,1)S(1)}, bf16[256,1024]{1,0:T(8,128)(2,1)S(1)}, f32[8,128,256]{2,1,0:T(8,128)S(1)}, bf16[1024,256]{1,0:T(8,128)(2...) custom-call(s32[96,128]{1,0:T(8,128)S(1)} %get-tuple-element.52.tab, ...), custom_call_target="tpu_custom_call" | custom-call | flops 2000000000 | bytes 1048576 | tf_op jit(solution)/shard_map/pallas_call | solution.py:486
  24.9 0.0 collective-permute-done.3.near_1
  25.0 1.0 %shard_map.69 = (bf16[1024,256]{1,0:T(8,128)(2,1)S(1)}, bf16[1024,256]{1,0:T(8,128)(2,1)S(1)}, f32[256,256]{1,0:T(8,128)S(1)}) custom-call(s32[96,128]{1,0:T(8,128)S(1)} %get-tuple-element.52.tab, bf16[2,8,128,128]{3,2,1,0:T(8,128)(2,1)S(1)} %get-tuple-element.64.a_high, bf16[2,8,128,128]{3,2,1,0:T(8,128)(2,1)S(1)} %get-tuple-element.65.a_low, ...), custom_call_target="tpu_custom_call" | custom-call | flops 2000000000 | bytes 1048576 | tf_op jit(solution)/shard_map/pallas_call | solution.py:486
  26.0 0.0 collective-permute-done.4.far_0
  26.0 1.1 %shard_map.70 = (f32[8,128,256]{2,1,0:T(8,128)S(1)}, bf16[1024,256]{1,0:T(8,128)(2,1)S(1)}, bf16[1024,256]{1,0:T(8,128)(2,1)S(1)}, f32[256,512]{1,0:T(8,128)S(1)}) custom-call(s32[96,128]{1,0:T(8,128)S(1)} %get-tuple-element.52.tab, bf16[2,8,128,128]{3,2,1,0:T(8,128)(2,1)S(1)} %get-tuple-element.64.a_high, ...), custom_call_target="tpu_custom_call" | custom-call | flops 1000000000 | bytes 1048576 | tf_op jit(solution)/shard_map/pallas_call | solution.py:486
  27.0 4.7 %collective-permute-done.5.far_1 = f32[4,2,128,128]{3,2,1,0:T(8,128)S(1)} collective-permute-done((f32[4,2,128,128]{3,2,1,0:T(8,128)S(1)}, f32[4,2,128,128]{3,2,1,0:T(8,128)S(1)}, u32[]{:S(2)}, u32[]{:S(2)}) %collective-permute-start.5) | collective-permute-done | bytes 524320 | tf_op jit(solution)/shard_map/ppermute | solution.py:27
  31.8 1.7 %shard_map.73 = (bf16[1024,256]{1,0:T(8,128)(2,1)S(1)}, bf16[1024,256]{1,0:T(8,128)(2,1)S(1)}, bf16[1024,256]{1,0:T(8,128)(2,1)S(1)}, bf16[1024,256]{1,0:T(8,128)(2,1)S(1)}, f32[256,512]{1,0:T(8,128)S(1)}) custom-call(s32[96,128]{1,0:T(8,128)S(1)} %get-tuple-element.52.tab, bf16[2,8,128,128]{3,2,1,0:T(8,128)(2,1)S(1)} %get-tuple-element.64.a_high, ...), custom_call_target="tpu_custom_call" | custom-call | flops 2000000000 | bytes 1048576 | tf_op jit(solution)/shard_map/pallas_call | solution.py:486
  33.5 2.5 %shard_map.76 = f32[256,1280]{1,0:T(8,128)S(1)} custom-call(s32[96,128]{1,0:T(8,128)S(1)} %get-tuple-element.52.tab, f32[8,2,128,128]{3,2,1,0:T(8,128)S(1)} %get-tuple-element.71.far, bf16[1024,256]{1,0:T(8,128)(2,1)S(1)} %get-tuple-element.73.refs_0_, bf16[1024,256]{1,0:T(8,128)(2,1)S(1)} %get-tuple-element.74.refs_1_, ...), custom_call_target="tpu_custom_call" | custom-call | flops 2000000000 | bytes 1048576 | tf_op jit(solution)/shard_map/pallas_call | solution.py:486
  36.0 0.1 collective-permute-start.6
  36.1 5.1 %collective-permute-start.9 = (f32[256,512]{1,0:T(8,128)S(1)}, f32[256,512]{1,0:T(8,128)S(1)}, u32[]{:S(2)}, u32[]{:S(2)}) collective-permute-start(f32[256,512]{1,0:T(8,128)S(1)} %get-tuple-element.98), channel_id=1, source_target_pairs={{1,2},{2,1},{3,4},{4,3},{5,6},{6,5},{7,8},{8,7},{9,10},{10,9},{11,... | collective-permute-start | bytes 1572872 | tf_op jit(solution)/shard_map/ppermute | solution.py:27
  41.2 2.1 %collective-permute-start.8 = (f32[256,512]{1,0:T(8,128)S(1)}, f32[256,512]{1,0:T(8,128)S(1)}, u32[]{:S(2)}, u32[]{:S(2)}) collective-permute-start(f32[256,512]{1,0:T(8,128)S(1)} %get-tuple-element.97), channel_id=1, source_target_pairs={{1,2},{2,1},{3,4},{4,3},{5,6},{6,5},{7,8},{8,7},{9,10},{10,9},{11,... | collective-permute-start | bytes 1572872 | tf_op jit(solution)/shard_map/ppermute | solution.py:27
  43.3 5.1 %collective-permute-start.7 = (f32[256,256]{1,0:T(8,128)S(1)}, f32[256,256]{1,0:T(8,128)S(1)}, u32[]{:S(2)}, u32[]{:S(2)}) collective-permute-start(f32[256,256]{1,0:T(8,128)S(1)} %get-tuple-element.96), channel_id=1, source_target_pairs={{1,2},{2,1},{3,4},{4,3},{5,6},{6,5},{7,8},{8,7},{9,10},{10,9},{11,... | collective-permute-start | bytes 786440 | tf_op jit(solution)/shard_map/ppermute | solution.py:27
  48.4 2.3 %shard_map.75.own = f32[256,1280]{1,0:T(8,128)S(1)} custom-call(f32[8,128,256]{2,1,0:T(8,128)S(1)} %get-tuple-element.61.own, bf16[1024,256]{1,0:T(8,128)(2,1)S(1)} %get-tuple-element.73.refs_0_, bf16[1024,256]{1,0:T(8,128)(2,1)S(1)} %get-tuple-element.74.refs_1_, bf16[1024,256]{1,0:T(8,128)(2,1)S(1)} %get-tuple-element.79.refs_2_, ...), custom_call_target="tpu_custom_call", output_to_operand_aliasing={{}: (11, {})} | custom-call | flops 2000000000 | bytes 1048576 | tf_op jit(solution)/shard_map/pallas_call | solution.py:486
  50.7 0.0 collective-permute-done.9.refs_0_
  50.7 1.1 %shard_map.77.refs_2_ = f32[2,14,128,128]{3,2,1,0:T(8,128)} custom-call(f32[2,128,128]{2,1,0:T(8,128)S(1)} %copy-done, f32[256,1280]{1,0:T(8,128)S(1)} %shard_map.75.own, f32[256,512]{1,0:T(8,128)S(1)} %collective-permute-done.9.refs_0_), custom_call_target="tpu_custom_call" | custom-call | flops 1000000000 | bytes 1048576 | tf_op jit(solution)/shard_map/pallas_call | solution.py:486
  51.8 4.0 %collective-permute-done.8.refs_1_ = f32[256,512]{1,0:T(8,128)S(1)} collective-permute-done((f32[256,512]{1,0:T(8,128)S(1)}, f32[256,512]{1,0:T(8,128)S(1)}, u32[]{:S(2)}, u32[]{:S(2)}) %collective-permute-start.8) | collective-permute-done | bytes 524320 | tf_op jit(solution)/shard_map/ppermute | solution.py:27
  55.8 1.3 %shard_map.78.refs_2_ = f32[2,14,128,128]{3,2,1,0:T(8,128)} custom-call(f32[2,128,128]{2,1,0:T(8,128)S(1)} %copy-done, f32[256,1280]{1,0:T(8,128)S(1)} %shard_map.75.own, f32[256,1280]{1,0:T(8,128)S(1)} %collective-permute-done.6.refs_0_, f32[256,512]{1,0:T(8,128)S(1)} %collective-permute-done.8.refs_1_, ...), custom_call_target="tpu_custom_call", output_to_operand_aliasing={{}: (4, {})} | custom-call | flops 1000000000 | bytes 1048576 | tf_op jit(solution)/shard_map/pallas_call | solution.py:486
  57.1 1.5 %collective-permute-done.7.refs_1_ = f32[256,256]{1,0:T(8,128)S(1)} collective-permute-done((f32[256,256]{1,0:T(8,128)S(1)}, f32[256,256]{1,0:T(8,128)S(1)}, u32[]{:S(2)}, u32[]{:S(2)}) %collective-permute-start.7) | collective-permute-done | bytes 262176 | tf_op jit(solution)/shard_map/ppermute | solution.py:27
  58.6 1.0 %shard_map.79 = f32[2,14,128,128]{3,2,1,0:T(8,128)} custom-call(f32[2,128,128]{2,1,0:T(8,128)S(1)} %copy-done, f32[256,1280]{1,0:T(8,128)S(1)} %shard_map.75.own, f32[256,1280]{1,0:T(8,128)S(1)} %collective-permute-done.6.refs_0_, f32[256,256]{1,0:T(8,128)S(1)} %collective-permute-done.7.refs_1_, ...), custom_call_target="tpu_custom_call", output_to_operand_aliasing={{}: (4, {})} | custom-call | flops 1000000000 | bytes 1048576 | tf_op jit(solution)/shard_map/pallas_call | solution.py:486
  (10 shorter events, 0.0 us)
Async XLA Ops:
  0.0 10.6 %copy-start.1 = (f32[8,4,128,128]{3,2,1,0:T(8,128)S(1)}, f32[8,4,128,128]{3,2,1,0:T(8,128)}, u32[]{:S(2)}) copy-start(f32[8,4,128,128]{3,2,1,0:T(8,128)} %a.1) | copy-start | bytes 6291460
  0.0 10.6 %copy-start.2 = (f32[8,128,128]{2,1,0:T(8,128)S(1)}, f32[8,128,128]{2,1,0:T(8,128)}, u32[]{:S(2)}) copy-start(f32[8,128,128]{2,1,0:T(8,128)} %dinv.5) | copy-start | bytes 1572868
  4.6 8.8 %collective-permute-start = (f32[4,128,128]{2,1,0:T(8,128)S(1)}, f32[4,128,128]{2,1,0:T(8,128)S(1)}, u32[]{:S(2)}, u32[]{:S(2)}) collective-permute-start(f32[4,128,128]{2,1,0:T(8,128)S(1)} %get-tuple-element.66), channel_id=1, source_target_pairs={{0,1},{1,0},{2,3},{3,2},{4,5},{5,4},{6,7},{7,6},{8,9},{9,8},{10,11... | collective-permute-start | bytes 786440 | tf_op jit(solution)/shard_map/ppermute | solution.py:27
  4.7 11.3 %collective-permute-start.1 = (f32[4,128,128]{2,1,0:T(8,128)S(1)}, f32[4,128,128]{2,1,0:T(8,128)S(1)}, u32[]{:S(2)}, u32[]{:S(2)}) collective-permute-start(f32[4,128,128]{2,1,0:T(8,128)S(1)} %get-tuple-element.69), channel_id=1, source_target_pairs={{1,2},{2,1},{3,4},{4,3},{5,6},{6,5},{7,8},{8,7},{9,10},{10,9},{11,... | collective-permute-start | bytes 786440 | tf_op jit(solution)/shard_map/ppermute | solution.py:27
  10.6 12.2 %collective-permute-start.2 = (f32[4,128,256]{2,1,0:T(8,128)S(1)}, f32[4,128,256]{2,1,0:T(8,128)S(1)}, u32[]{:S(2)}, u32[]{:S(2)}) collective-permute-start(f32[4,128,256]{2,1,0:T(8,128)S(1)} %get-tuple-element.72), channel_id=1, source_target_pairs={{0,1},{1,0},{2,3},{3,2},{4,5},{5,4},{6,7},{7,6},{8,9},{9,8},{10,11... | collective-permute-start | bytes 1572872 | tf_op jit(solution)/shard_map/ppermute | solution.py:27
  10.6 14.4 %collective-permute-start.3 = (f32[4,128,256]{2,1,0:T(8,128)S(1)}, f32[4,128,256]{2,1,0:T(8,128)S(1)}, u32[]{:S(2)}, u32[]{:S(2)}) collective-permute-start(f32[4,128,256]{2,1,0:T(8,128)S(1)} %get-tuple-element.78), channel_id=1, source_target_pairs={{1,2},{2,1},{3,4},{4,3},{5,6},{6,5},{7,8},{8,7},{9,10},{10,9},{11,... | collective-permute-start | bytes 1572872 | tf_op jit(solution)/shard_map/ppermute | solution.py:27
  16.8 9.2 %collective-permute-start.4 = (f32[4,2,128,128]{3,2,1,0:T(8,128)S(1)}, f32[4,2,128,128]{3,2,1,0:T(8,128)S(1)}, u32[]{:S(2)}, u32[]{:S(2)}) collective-permute-start(f32[4,2,128,128]{3,2,1,0:T(8,128)S(1)} %get-tuple-element.81), channel_id=1, source_target_pairs={{0,1},{1,0},{2,3},{3,2},{4,5},{5,4},{6,7},{7,6},{8,9},{9,8},{10,11... | collective-permute-start | bytes 1572872 | tf_op jit(solution)/shard_map/ppermute | solution.py:27
  17.6 14.1 %collective-permute-start.5 = (f32[4,2,128,128]{3,2,1,0:T(8,128)S(1)}, f32[4,2,128,128]{3,2,1,0:T(8,128)S(1)}, u32[]{:S(2)}, u32[]{:S(2)}) collective-permute-start(f32[4,2,128,128]{3,2,1,0:T(8,128)S(1)} %get-tuple-element.70.far_1), channel_id=1, source_target_pairs={{1,2},{2,1},{3,4},{4,3},{5,6},{6,5},{7,8},{8,7},{9,10},{10,9},{11,... | collective-permute-start | bytes 1572872 | tf_op jit(solution)/shard_map/ppermute | solution.py:27
  36.0 19.8 %collective-permute-start.6 = (f32[256,1280]{1,0:T(8,128)S(1)}, f32[256,1280]{1,0:T(8,128)S(1)}, u32[]{:S(2)}, u32[]{:S(2)}) collective-permute-start(f32[256,1280]{1,0:T(8,128)S(1)} %shard_map.76), channel_id=1, source_target_pairs={{0,1},{1,0},{2,3},{3,2},{4,5},{5,4},{6,7},{7,6},{8,9},{9,8},{10,11... | collective-permute-start | bytes 3932168 | tf_op jit(solution)/shard_map/ppermute | solution.py:27
  36.1 14.6 %collective-permute-start.9 = (f32[256,512]{1,0:T(8,128)S(1)}, f32[256,512]{1,0:T(8,128)S(1)}, u32[]{:S(2)}, u32[]{:S(2)}) collective-permute-start(f32[256,512]{1,0:T(8,128)S(1)} %get-tuple-element.98), channel_id=1, source_target_pairs={{1,2},{2,1},{3,4},{4,3},{5,6},{6,5},{7,8},{8,7},{9,10},{10,9},{11,... | collective-permute-start | bytes 1572872 | tf_op jit(solution)/shard_map/ppermute | solution.py:27
  41.2 14.6 %collective-permute-start.8 = (f32[256,512]{1,0:T(8,128)S(1)}, f32[256,512]{1,0:T(8,128)S(1)}, u32[]{:S(2)}, u32[]{:S(2)}) collective-permute-start(f32[256,512]{1,0:T(8,128)S(1)} %get-tuple-element.97), channel_id=1, source_target_pairs={{1,2},{2,1},{3,4},{4,3},{5,6},{6,5},{7,8},{8,7},{9,10},{10,9},{11,... | collective-permute-start | bytes 1572872 | tf_op jit(solution)/shard_map/ppermute | solution.py:27
  43.3 15.3 %collective-permute-start.7 = (f32[256,256]{1,0:T(8,128)S(1)}, f32[256,256]{1,0:T(8,128)S(1)}, u32[]{:S(2)}, u32[]{:S(2)}) collective-permute-start(f32[256,256]{1,0:T(8,128)S(1)} %get-tuple-element.96), channel_id=1, source_target_pairs={{1,2},{2,1},{3,4},{4,3},{5,6},{6,5},{7,8},{8,7},{9,10},{10,9},{11,... | collective-permute-start | bytes 786440 | tf_op jit(solution)/shard_map/ppermute | solution.py:27
  48.4 2.3 %copy-start = (f32[2,128,128]{2,1,0:T(8,128)S(1)}, f32[2,128,128]{2,1,0:T(8,128)}, u32[]{:S(2)}) copy-start(f32[2,128,128]{2,1,0:T(8,128)} %inverse.5) | copy-start | bytes 393220

commit v2 on v0

--- a/solution.py
+++ b/solution.py
@@ -67,8 +67,8 @@
     cols, agg, rank, dinv, a, sem,
 ):
     early = [
-        pltpu.make_async_copy(dinv_hbm, dinv, sem.at[5]),
-        pltpu.make_async_copy(a_hbm, a, sem.at[6]),
+        pltpu.make_async_copy(dinv_hbm, dinv, sem.at[4]),
+        pltpu.make_async_copy(a_hbm, a, sem.at[5]),
     ]
 
     rows, width = t.shape[0], t.shape[0] // 2
@@ -87,9 +87,10 @@
         )
         for i, slab in enumerate(slabs)
     ]
-    copies += [pltpu.make_async_copy(t_hbm, t, sem.at[3]), pltpu.make_async_copy(agg_hbm, agg, sem.at[4])]
-    for i, copy in enumerate(copies):
-        copy.start(priority=1 if i == 3 else 0)
+    t_rows = [pltpu.make_async_copy(t_hbm.at[r], t.at[r], sem.at[6 + r]) for r in range(rows)]
+    copies.append(pltpu.make_async_copy(agg_hbm, agg, sem.at[3]))
+    for copy in copies[:2] + t_rows + copies[2:]:
+        copy.start()
 
     def col(i, r, k):
         return cols[i * chunk + k * ROW_CHUNK + ((slabs[i] * rows) & (ROW_CHUNK - 1)) + r]
@@ -115,12 +116,13 @@
     rank_rows(0, 3, 0)
     rank_rows(1, 2, 2)
     sent_1, sent_0 = jnp.where(side == ABOVE, 0, 2), jnp.where(side == ABOVE, 2, 0)
-    copies[3].wait()
+    for copy in t_rows:
+        copy.wait()
     for j in range(width):
         t_1[j] = t[ranked(sent_1 + 1, j)]
         t_0[j] = t[ranked(sent_0 + 1, j)]
     copies[2].wait()
-    copies[4].wait()
+    copies[3].wait()
     rank_rows(2, 2, 4)
     rank_rows(2, 3, 6)
     for j in range(width):
@@ -501,7 +503,7 @@
             pltpu.SMEM((8 * rows,), jnp.int32),
             (dinv.shape, F32),
             (a.shape, F32),
-            pltpu.SemaphoreType.DMA((7,)),
+            pltpu.SemaphoreType.DMA((6 + rows,)),
         ],
         micros=3,
         in_hbm=(0, 1, 2, 3, 4),

time: 59.8 us -> 59.9 us (level)
  no operation moved by 1% of the time
where the time goes in v2:
time: 59.9 us; the launch traced here: 59.7 us
  starting transfers between devices  26.4 us (44%)
  Pallas kernels  20.7 us (35%)
  waiting for transfers between devices  12.4 us (21%)
    ppermute x10, starting transfers between devices, exchanged(): return lax.ppermute(value, AXES, pairs)  26.4 us
    pallas_call x16, Pallas kernels, call(): pl.pallas_call(body, out_shape=outs, in_specs=specs(ins, in_hbm), out_spe...  20.7 us
    ppermute x10, waiting for transfers between devices, exchanged(): return lax.ppermute(value, AXES, pairs)  12.4 us
  transfers between devices with their start and end apart: 10, of which 4 were waited for; matrix products, arithmetic and copies ran while one was open for 0% of the time, Pallas kernels for 18%

profile of v2, /device:TPU:0, one launch (start us, length us, event | category | flops | bytes accessed | tf_op | source)
XLA Modules:
  0.0 59.7 jit_solution(6127362496730104358)
XLA Ops:
  0.0 4.6 %shard_map.64 = (s32[96,128]{1,0:T(8,128)S(1)}, f32[4,128,128]{2,1,0:T(8,128)S(1)}, f32[4,128,128]{2,1,0:T(8,128)S(1)}, f32[8,128,128]{2,1,0:T(8,128)S(1)}, f32[...) custom-call(s32[4096]{0:T(1024)} %bitcast.5, ...), custom_call_target="tpu_custom_call" | custom-call | flops 3000000000 | bytes 1048576 | tf_op jit(solution)/shard_map/pallas_call | solution.py:472
  4.6 0.1 collective-permute-start
  4.7 5.9 %collective-permute-start.1 = (f32[4,128,128]{2,1,0:T(8,128)S(1)}, f32[4,128,128]{2,1,0:T(8,128)S(1)}, u32[]{:S(2)}, u32[]{:S(2)}) collective-permute-start(f32[4,128,128]{2,1,0:T(8,128)S(1)} %get-tuple-element.69), channel_id=1, source_target_pairs={{1,2},{2,1},{3,4},{4,3},{5,6},{6,5},{7,8},{8,7},{9,10},{10,9},{11,... | collective-permute-start | bytes 786440 | tf_op jit(solution)/shard_map/ppermute | solution.py:27
  10.6 0.0 collective-permute-start.2
  10.6 2.8 %collective-permute-start.3 = (f32[4,128,256]{2,1,0:T(8,128)S(1)}, f32[4,128,256]{2,1,0:T(8,128)S(1)}, u32[]{:S(2)}, u32[]{:S(2)}) collective-permute-start(f32[4,128,256]{2,1,0:T(8,128)S(1)} %get-tuple-element.78), channel_id=1, source_target_pairs={{1,2},{2,1},{3,4},{4,3},{5,6},{6,5},{7,8},{8,7},{9,10},{10,9},{11,... | collective-permute-start | bytes 1572872 | tf_op jit(solution)/shard_map/ppermute | solution.py:27
  13.4 0.0 collective-permute-done.t_0
  13.4 0.5 shard_map.66
  13.9 2.1 %collective-permute-done.1.t_1 = f32[4,128,128]{2,1,0:T(8,128)S(1)} collective-permute-done((f32[4,128,128]{2,1,0:T(8,128)S(1)}, f32[4,128,128]{2,1,0:T(8,128)S(1)}, u32[]{:S(2)}, u32[]{:S(2)}) %collective-permute-start.1) | collective-permute-done | bytes 262176 | tf_op jit(solution)/shard_map/ppermute | solution.py:27
  16.0 0.8 %shard_map.67 = (f32[4,2,128,128]{3,2,1,0:T(8,128)S(1)}, f32[8,2,128,128]{3,2,1,0:T(8,128)S(1)}) custom-call(s32[96,128]{1,0:T(8,128)S(1)} %get-tuple-element.52.tab, bf16[2,8,128,128]{3,2,1,0:T(8,128)(2,1)S(1)} %get-tuple-element.64.a_high, bf16[2,8,128,128]{3,2,1,0:T(8,128)(2,1)S(1)} %get-tuple-element.65.a_low, f32[8,128,128]{2,1,0:T(8,128)S(1)} %copy-done.2, ...), custom_call_target="tpu_custom_call" | custom-call | flops 1000000000 | bytes 1048576 | tf_op jit(solution)/shard_map/pallas_call | solution.py:472
  16.8 0.1 collective-permute-start.4
  16.9 0.8 %shard_map.71 = (f32[8,128,256]{2,1,0:T(8,128)S(1)}, bf16[4,128,128]{2,1,0:T(8,128)(2,1)S(1)}, bf16[4,128,128]{2,1,0:T(8,128)(2,1)S(1)}) custom-call(s32[96,128]{1,0:T(8,128)S(1)} %get-tuple-element.52.tab, bf16[8,128,256]{2,1,0:T(8,128)(2,1)S(1)} %get-tuple-element.62.a01_high, bf16[8,128,256]{2,1,0:T(8,128)(2,1)S(1)} %get-tuple-element.63.a01_low, ...), custom_call_target="tpu_custom_call" | custom-call | flops 1000000000 | bytes 1048576 | tf_op jit(solution)/shard_map/pallas_call | solution.py:472
  17.7 5.1 %collective-permute-start.5 = (f32[4,2,128,128]{3,2,1,0:T(8,128)S(1)}, f32[4,2,128,128]{3,2,1,0:T(8,128)S(1)}, u32[]{:S(2)}, u32[]{:S(2)}) collective-permute-start(f32[4,2,128,128]{3,2,1,0:T(8,128)S(1)} %get-tuple-element.70.far_1), channel_id=1, source_target_pairs={{1,2},{2,1},{3,4},{4,3},{5,6},{6,5},{7,8},{8,7},{9,10},{10,9},{11,... | collective-permute-start | bytes 1572872 | tf_op jit(solution)/shard_map/ppermute | solution.py:27
  22.8 0.0 collective-permute-done.2.near_0
  22.8 2.2 %shard_map.68 = (bf16[256,1024]{1,0:T(8,128)(2,1)S(1)}, bf16[256,1024]{1,0:T(8,128)(2,1)S(1)}, f32[8,128,256]{2,1,0:T(8,128)S(1)}, bf16[1024,256]{1,0:T(8,128)(2...) custom-call(s32[96,128]{1,0:T(8,128)S(1)} %get-tuple-element.52.tab, ...), custom_call_target="tpu_custom_call" | custom-call | flops 2000000000 | bytes 1048576 | tf_op jit(solution)/shard_map/pallas_call | solution.py:472
  25.0 0.0 collective-permute-done.3.near_1
  25.0 1.0 %shard_map.69 = (bf16[1024,256]{1,0:T(8,128)(2,1)S(1)}, bf16[1024,256]{1,0:T(8,128)(2,1)S(1)}, f32[256,256]{1,0:T(8,128)S(1)}) custom-call(s32[96,128]{1,0:T(8,128)S(1)} %get-tuple-element.52.tab, bf16[2,8,128,128]{3,2,1,0:T(8,128)(2,1)S(1)} %get-tuple-element.64.a_high, bf16[2,8,128,128]{3,2,1,0:T(8,128)(2,1)S(1)} %get-tuple-element.65.a_low, ...), custom_call_target="tpu_custom_call" | custom-call | flops 2000000000 | bytes 1048576 | tf_op jit(solution)/shard_map/pallas_call | solution.py:472
  26.0 1.1 %shard_map.70 = (f32[8,128,256]{2,1,0:T(8,128)S(1)}, bf16[1024,256]{1,0:T(8,128)(2,1)S(1)}, bf16[1024,256]{1,0:T(8,128)(2,1)S(1)}, f32[256,512]{1,0:T(8,128)S(1)}) custom-call(s32[96,128]{1,0:T(8,128)S(1)} %get-tuple-element.52.tab, bf16[2,8,128,128]{3,2,1,0:T(8,128)(2,1)S(1)} %get-tuple-element.64.a_high, ...), custom_call_target="tpu_custom_call" | custom-call | flops 1000000000 | bytes 1048576 | tf_op jit(solution)/shard_map/pallas_call | solution.py:472
  27.1 4.7 %collective-permute-done.5.far_1 = f32[4,2,128,128]{3,2,1,0:T(8,128)S(1)} collective-permute-done((f32[4,2,128,128]{3,2,1,0:T(8,128)S(1)}, f32[4,2,128,128]{3,2,1,0:T(8,128)S(1)}, u32[]{:S(2)}, u32[]{:S(2)}) %collective-permute-start.5) | collective-permute-done | bytes 524320 | tf_op jit(solution)/shard_map/ppermute | solution.py:27
  31.8 1.7 %shard_map.73 = (bf16[1024,256]{1,0:T(8,128)(2,1)S(1)}, bf16[1024,256]{1,0:T(8,128)(2,1)S(1)}, bf16[1024,256]{1,0:T(8,128)(2,1)S(1)}, bf16[1024,256]{1,0:T(8,128)(2,1)S(1)}, f32[256,512]{1,0:T(8,128)S(1)}) custom-call(s32[96,128]{1,0:T(8,128)S(1)} %get-tuple-element.52.tab, bf16[2,8,128,128]{3,2,1,0:T(8,128)(2,1)S(1)} %get-tuple-element.64.a_high, ...), custom_call_target="tpu_custom_call" | custom-call | flops 2000000000 | bytes 1048576 | tf_op jit(solution)/shard_map/pallas_call | solution.py:472
  33.5 2.5 %shard_map.76 = f32[256,1280]{1,0:T(8,128)S(1)} custom-call(s32[96,128]{1,0:T(8,128)S(1)} %get-tuple-element.52.tab, f32[8,2,128,128]{3,2,1,0:T(8,128)S(1)} %get-tuple-element.71.far, bf16[1024,256]{1,0:T(8,128)(2,1)S(1)} %get-tuple-element.73.refs_0_, bf16[1024,256]{1,0:T(8,128)(2,1)S(1)} %get-tuple-element.74.refs_1_, ...), custom_call_target="tpu_custom_call" | custom-call | flops 2000000000 | bytes 1048576 | tf_op jit(solution)/shard_map/pallas_call | solution.py:472
  36.0 0.1 collective-permute-start.6
  36.1 5.1 %collective-permute-start.9 = (f32[256,512]{1,0:T(8,128)S(1)}, f32[256,512]{1,0:T(8,128)S(1)}, u32[]{:S(2)}, u32[]{:S(2)}) collective-permute-start(f32[256,512]{1,0:T(8,128)S(1)} %get-tuple-element.98), channel_id=1, source_target_pairs={{1,2},{2,1},{3,4},{4,3},{5,6},{6,5},{7,8},{8,7},{9,10},{10,9},{11,... | collective-permute-start | bytes 1572872 | tf_op jit(solution)/shard_map/ppermute | solution.py:27
  41.2 2.1 %collective-permute-start.8 = (f32[256,512]{1,0:T(8,128)S(1)}, f32[256,512]{1,0:T(8,128)S(1)}, u32[]{:S(2)}, u32[]{:S(2)}) collective-permute-start(f32[256,512]{1,0:T(8,128)S(1)} %get-tuple-element.97), channel_id=1, source_target_pairs={{1,2},{2,1},{3,4},{4,3},{5,6},{6,5},{7,8},{8,7},{9,10},{10,9},{11,... | collective-permute-start | bytes 1572872 | tf_op jit(solution)/shard_map/ppermute | solution.py:27
  43.3 5.1 %collective-permute-start.7 = (f32[256,256]{1,0:T(8,128)S(1)}, f32[256,256]{1,0:T(8,128)S(1)}, u32[]{:S(2)}, u32[]{:S(2)}) collective-permute-start(f32[256,256]{1,0:T(8,128)S(1)} %get-tuple-element.96), channel_id=1, source_target_pairs={{1,2},{2,1},{3,4},{4,3},{5,6},{6,5},{7,8},{8,7},{9,10},{10,9},{11,... | collective-permute-start | bytes 786440 | tf_op jit(solution)/shard_map/ppermute | solution.py:27
  48.4 2.3 %shard_map.75.own = f32[256,1280]{1,0:T(8,128)S(1)} custom-call(f32[8,128,256]{2,1,0:T(8,128)S(1)} %get-tuple-element.61.own, bf16[1024,256]{1,0:T(8,128)(2,1)S(1)} %get-tuple-element.73.refs_0_, bf16[1024,256]{1,0:T(8,128)(2,1)S(1)} %get-tuple-element.74.refs_1_, bf16[1024,256]{1,0:T(8,128)(2,1)S(1)} %get-tuple-element.79.refs_2_, ...), custom_call_target="tpu_custom_call", output_to_operand_aliasing={{}: (11, {})} | custom-call | flops 2000000000 | bytes 1048576 | tf_op jit(solution)/shard_map/pallas_call | solution.py:472
  50.7 0.0 collective-permute-done.9.refs_0_
  50.7 1.1 %shard_map.77.refs_2_ = f32[2,14,128,128]{3,2,1,0:T(8,128)} custom-call(f32[2,128,128]{2,1,0:T(8,128)S(1)} %copy-done, f32[256,1280]{1,0:T(8,128)S(1)} %shard_map.75.own, f32[256,512]{1,0:T(8,128)S(1)} %collective-permute-done.9.refs_0_), custom_call_target="tpu_custom_call" | custom-call | flops 1000000000 | bytes 1048576 | tf_op jit(solution)/shard_map/pallas_call | solution.py:472
  51.8 4.0 %collective-permute-done.8.refs_1_ = f32[256,512]{1,0:T(8,128)S(1)} collective-permute-done((f32[256,512]{1,0:T(8,128)S(1)}, f32[256,512]{1,0:T(8,128)S(1)}, u32[]{:S(2)}, u32[]{:S(2)}) %collective-permute-start.8) | collective-permute-done | bytes 524320 | tf_op jit(solution)/shard_map/ppermute | solution.py:27
  55.8 0.0 collective-permute-done.6.refs_0_
  55.8 1.3 %shard_map.78.refs_2_ = f32[2,14,128,128]{3,2,1,0:T(8,128)} custom-call(f32[2,128,128]{2,1,0:T(8,128)S(1)} %copy-done, f32[256,1280]{1,0:T(8,128)S(1)} %shard_map.75.own, f32[256,1280]{1,0:T(8,128)S(1)} %collective-permute-done.6.refs_0_, f32[256,512]{1,0:T(8,128)S(1)} %collective-permute-done.8.refs_1_, ...), custom_call_target="tpu_custom_call", output_to_operand_aliasing={{}: (4, {})} | custom-call | flops 1000000000 | bytes 1048576 | tf_op jit(solution)/shard_map/pallas_call | solution.py:472
  57.1 1.5 %collective-permute-done.7.refs_1_ = f32[256,256]{1,0:T(8,128)S(1)} collective-permute-done((f32[256,256]{1,0:T(8,128)S(1)}, f32[256,256]{1,0:T(8,128)S(1)}, u32[]{:S(2)}, u32[]{:S(2)}) %collective-permute-start.7) | collective-permute-done | bytes 262176 | tf_op jit(solution)/shard_map/ppermute | solution.py:27
  58.6 1.0 %shard_map.79 = f32[2,14,128,128]{3,2,1,0:T(8,128)} custom-call(f32[2,128,128]{2,1,0:T(8,128)S(1)} %copy-done, f32[256,1280]{1,0:T(8,128)S(1)} %shard_map.75.own, f32[256,1280]{1,0:T(8,128)S(1)} %collective-permute-done.6.refs_0_, f32[256,256]{1,0:T(8,128)S(1)} %collective-permute-done.7.refs_1_, ...), custom_call_target="tpu_custom_call", output_to_operand_aliasing={{}: (4, {})} | custom-call | flops 1000000000 | bytes 1048576 | tf_op jit(solution)/shard_map/pallas_call | solution.py:472
  (10 shorter events, 0.0 us)
Async XLA Ops:
  0.0 10.6 %copy-start.1 = (f32[8,4,128,128]{3,2,1,0:T(8,128)S(1)}, f32[8,4,128,128]{3,2,1,0:T(8,128)}, u32[]{:S(2)}) copy-start(f32[8,4,128,128]{3,2,1,0:T(8,128)} %a.1) | copy-start | bytes 6291460
  0.0 10.6 %copy-start.2 = (f32[8,128,128]{2,1,0:T(8,128)S(1)}, f32[8,128,128]{2,1,0:T(8,128)}, u32[]{:S(2)}) copy-start(f32[8,128,128]{2,1,0:T(8,128)} %dinv.5) | copy-start | bytes 1572868
  4.6 8.8 %collective-permute-start = (f32[4,128,128]{2,1,0:T(8,128)S(1)}, f32[4,128,128]{2,1,0:T(8,128)S(1)}, u32[]{:S(2)}, u32[]{:S(2)}) collective-permute-start(f32[4,128,128]{2,1,0:T(8,128)S(1)} %get-tuple-element.66), channel_id=1, source_target_pairs={{0,1},{1,0},{2,3},{3,2},{4,5},{5,4},{6,7},{7,6},{8,9},{9,8},{10,11... | collective-permute-start | bytes 786440 | tf_op jit(solution)/shard_map/ppermute | solution.py:27
  4.7 11.3 %collective-permute-start.1 = (f32[4,128,128]{2,1,0:T(8,128)S(1)}, f32[4,128,128]{2,1,0:T(8,128)S(1)}, u32[]{:S(2)}, u32[]{:S(2)}) collective-permute-start(f32[4,128,128]{2,1,0:T(8,128)S(1)} %get-tuple-element.69), channel_id=1, source_target_pairs={{1,2},{2,1},{3,4},{4,3},{5,6},{6,5},{7,8},{8,7},{9,10},{10,9},{11,... | collective-permute-start | bytes 786440 | tf_op jit(solution)/shard_map/ppermute | solution.py:27
  10.6 12.2 %collective-permute-start.2 = (f32[4,128,256]{2,1,0:T(8,128)S(1)}, f32[4,128,256]{2,1,0:T(8,128)S(1)}, u32[]{:S(2)}, u32[]{:S(2)}) collective-permute-start(f32[4,128,256]{2,1,0:T(8,128)S(1)} %get-tuple-element.72), channel_id=1, source_target_pairs={{0,1},{1,0},{2,3},{3,2},{4,5},{5,4},{6,7},{7,6},{8,9},{9,8},{10,11... | collective-permute-start | bytes 1572872 | tf_op jit(solution)/shard_map/ppermute | solution.py:27
  10.6 14.4 %collective-permute-start.3 = (f32[4,128,256]{2,1,0:T(8,128)S(1)}, f32[4,128,256]{2,1,0:T(8,128)S(1)}, u32[]{:S(2)}, u32[]{:S(2)}) collective-permute-start(f32[4,128,256]{2,1,0:T(8,128)S(1)} %get-tuple-element.78), channel_id=1, source_target_pairs={{1,2},{2,1},{3,4},{4,3},{5,6},{6,5},{7,8},{8,7},{9,10},{10,9},{11,... | collective-permute-start | bytes 1572872 | tf_op jit(solution)/shard_map/ppermute | solution.py:27
  16.8 9.2 %collective-permute-start.4 = (f32[4,2,128,128]{3,2,1,0:T(8,128)S(1)}, f32[4,2,128,128]{3,2,1,0:T(8,128)S(1)}, u32[]{:S(2)}, u32[]{:S(2)}) collective-permute-start(f32[4,2,128,128]{3,2,1,0:T(8,128)S(1)} %get-tuple-element.81), channel_id=1, source_target_pairs={{0,1},{1,0},{2,3},{3,2},{4,5},{5,4},{6,7},{7,6},{8,9},{9,8},{10,11... | collective-permute-start | bytes 1572872 | tf_op jit(solution)/shard_map/ppermute | solution.py:27
  17.7 14.1 %collective-permute-start.5 = (f32[4,2,128,128]{3,2,1,0:T(8,128)S(1)}, f32[4,2,128,128]{3,2,1,0:T(8,128)S(1)}, u32[]{:S(2)}, u32[]{:S(2)}) collective-permute-start(f32[4,2,128,128]{3,2,1,0:T(8,128)S(1)} %get-tuple-element.70.far_1), channel_id=1, source_target_pairs={{1,2},{2,1},{3,4},{4,3},{5,6},{6,5},{7,8},{8,7},{9,10},{10,9},{11,... | collective-permute-start | bytes 1572872 | tf_op jit(solution)/shard_map/ppermute | solution.py:27
  36.0 19.8 %collective-permute-start.6 = (f32[256,1280]{1,0:T(8,128)S(1)}, f32[256,1280]{1,0:T(8,128)S(1)}, u32[]{:S(2)}, u32[]{:S(2)}) collective-permute-start(f32[256,1280]{1,0:T(8,128)S(1)} %shard_map.76), channel_id=1, source_target_pairs={{0,1},{1,0},{2,3},{3,2},{4,5},{5,4},{6,7},{7,6},{8,9},{9,8},{10,11... | collective-permute-start | bytes 3932168 | tf_op jit(solution)/shard_map/ppermute | solution.py:27
  36.1 14.6 %collective-permute-start.9 = (f32[256,512]{1,0:T(8,128)S(1)}, f32[256,512]{1,0:T(8,128)S(1)}, u32[]{:S(2)}, u32[]{:S(2)}) collective-permute-start(f32[256,512]{1,0:T(8,128)S(1)} %get-tuple-element.98), channel_id=1, source_target_pairs={{1,2},{2,1},{3,4},{4,3},{5,6},{6,5},{7,8},{8,7},{9,10},{10,9},{11,... | collective-permute-start | bytes 1572872 | tf_op jit(solution)/shard_map/ppermute | solution.py:27
  41.2 14.6 %collective-permute-start.8 = (f32[256,512]{1,0:T(8,128)S(1)}, f32[256,512]{1,0:T(8,128)S(1)}, u32[]{:S(2)}, u32[]{:S(2)}) collective-permute-start(f32[256,512]{1,0:T(8,128)S(1)} %get-tuple-element.97), channel_id=1, source_target_pairs={{1,2},{2,1},{3,4},{4,3},{5,6},{6,5},{7,8},{8,7},{9,10},{10,9},{11,... | collective-permute-start | bytes 1572872 | tf_op jit(solution)/shard_map/ppermute | solution.py:27
  43.3 15.3 %collective-permute-start.7 = (f32[256,256]{1,0:T(8,128)S(1)}, f32[256,256]{1,0:T(8,128)S(1)}, u32[]{:S(2)}, u32[]{:S(2)}) collective-permute-start(f32[256,256]{1,0:T(8,128)S(1)} %get-tuple-element.96), channel_id=1, source_target_pairs={{1,2},{2,1},{3,4},{4,3},{5,6},{6,5},{7,8},{8,7},{9,10},{10,9},{11,... | collective-permute-start | bytes 786440 | tf_op jit(solution)/shard_map/ppermute | solution.py:27
  48.4 2.3 %copy-start = (f32[2,128,128]{2,1,0:T(8,128)S(1)}, f32[2,128,128]{2,1,0:T(8,128)}, u32[]{:S(2)}) copy-start(f32[2,128,128]{2,1,0:T(8,128)} %inverse.5) | copy-start | bytes 393220

commit v3 on v0

--- a/solution.py
+++ b/solution.py
@@ -63,7 +63,7 @@
 
 def load_kernel(
     devices, cols_hbm, agg_hbm, t_hbm, dinv_hbm, a_hbm,
-    tab, t_0, t_1, t, near_0, near_1, own, a_high, a_low, a01_high, a01_low,
+    tab, t_0, t_1, t, near_0, near_1, own, a_high, a_low, a01_high, a01_low, m_high, m_low,
     cols, agg, rank, dinv, a, sem,
 ):
     early = [
@@ -88,8 +88,13 @@
         for i, slab in enumerate(slabs)
     ]
     copies += [pltpu.make_async_copy(t_hbm, t, sem.at[3]), pltpu.make_async_copy(agg_hbm, agg, sem.at[4])]
-    for i, copy in enumerate(copies):
-        copy.start(priority=1 if i == 3 else 0)
+    for copy in copies:
+        copy.start()
+
+    @pl.when(far_partner())
+    def _():
+        for copy in early:
+            copy.start()
 
     def col(i, r, k):
         return cols[i * chunk + k * ROW_CHUNK + ((slabs[i] * rows) & (ROW_CHUNK - 1)) + r]
@@ -141,10 +146,8 @@
     @pl.when(far_partner())
     def _():
         for copy in early:
-            copy.start()
-        for copy in early:
             copy.wait()
-        near_blocks(tab, a, t, dinv, near_0, near_1, own, a_high, a_low, a01_high, a01_low)
+        near_blocks(tab, a, t, dinv, near_0, near_1, own, a_high, a_low, a01_high, a01_low, m_high, m_low)
 
 
 def put(value, label, column):
@@ -179,7 +182,7 @@
     return jnp.concatenate([ref[place] for place in places], axis=0)
 
 
-def near_blocks(tab, a, t, dinv, near_0, near_1, own, a_high, a_low, a01_high, a01_low):
+def near_blocks(tab, a, t, dinv, near_0, near_1, own, a_high, a_low, a01_high, a01_low, m_high, m_low):
     rows, width = own.shape[0], near_1.shape[0]
     for u, value in enumerate(near_tiles(tab, a, t, dinv, range(rows))):
         own[u] = value
@@ -192,10 +195,18 @@
         a01_high[u], a01_low[u] = split(jnp.concatenate([a[row, 0], a[row, 1]], axis=1))
         for which in (BELOW, ABOVE):
             a_high[which, u], a_low[which, u] = split(a[row, 2 + which])
+    makers = []
+    for u in range(width):
+        wide_high, wide_low = (jnp.concatenate([x[BELOW, u], x[ABOVE, u]], axis=1) for x in (a_high, a_low))
+        makers.append(-OMEGA * dot3k(*split(dinv[entry(tab, ROW + u)]), wide_high, wide_low))
+    block = t.shape[1]
+    for u in range(width):
+        for which in (BELOW, ABOVE):
+            m_high[which, u], m_low[which, u] = split(makers[u][:, which * block : (which + 1) * block])
 
 
 def near_kernel(tab, a, t, dinv, *refs):
-    pl.when(jnp.logical_not(far_partner()))(lambda: near_blocks(tab, a, t, dinv, *refs[7:]))
+    pl.when(jnp.logical_not(far_partner()))(lambda: near_blocks(tab, a, t, dinv, *refs[9:]))
 
 
 def far_blocks(tab, a_high, a_low, dinv, t_high, t_low, order):
@@ -217,22 +228,13 @@
         high[j], low[j] = split(value[j])
 
 
-def far_sent_kernel(tab, a_high, a_low, dinv, t_0, far_1, t_high, t_low):
+def far_sent_kernel(tab, m_high, m_low, t_0, far_1, t_high, t_low):
     side = pair_side()
-    block = dinv.shape[1]
     split_rows(t_0, t_high, t_low)
-    order = range(far_1.shape[0])
-    prods = []
-    for u in order:
+    for u in range(far_1.shape[0]):
         pos = entry(tab, POS2 + 8 * side + u)
-        high, low = split(dot3k(a_high[side, u], a_low[side, u], t_high[pos], t_low[pos]))
-        prods.append(
-            (jnp.concatenate([high, a_high[1 - side, u]], axis=1), jnp.concatenate([low, a_low[1 - side, u]], axis=1))
-        )
-    for u in order:
-        both = -OMEGA * dot3k(*split(dinv[entry(tab, ROW + u)]), *prods[u])
-        far_1[u, side] = both[:, :block]
-        far_1[u, 1 - side] = both[:, block:]
+        far_1[u, side] = dot3k(m_high[side, u], m_low[side, u], t_high[pos], t_low[pos])
+        far_1[u, 1 - side] = m_high[1 - side, u].astype(F32) + m_low[1 - side, u].astype(F32)
 
 
 def store_turned(trans, label, place, value):
@@ -491,6 +493,7 @@
     cols = a_cols.reshape(-1, ROW_CHUNK, 4).transpose(0, 2, 1).reshape(-1)
 
     near_shapes = [tile, tile, full(rows, block, half)] + pair(2, rows, block, block) + pair(rows, block, half)
+    near_shapes += pair(2, width, block, block)
     tab, t_0, t_1, t, *near = call(
         functools.partial(load_kernel, devices),
         [shape((TAB, LANES), jnp.int32)] + [full(width, block, block)] * 2 + [full(*t_blocks.shape)] + near_shapes,
@@ -508,13 +511,13 @@
     )
     t_0 = exchanged(t_0, 0)
     t_1 = exchanged(t_1, 1)
-    near_0, near_1, own, a23_high, a23_low, a01_high, a01_low = call(
-        near_kernel, near_shapes, [tab, a, t, dinv, *near], micros=2, aliases={4 + i: i for i in range(7)}
+    near_0, near_1, own, a23_high, a23_low, a01_high, a01_low, m_high, m_low = call(
+        near_kernel, near_shapes, [tab, a, t, dinv, *near], micros=2, aliases={4 + i: i for i in range(9)}
     )
     near_0 = exchanged(near_0, 0)
     sent = full(width, 2, block, block)
     far_1, t0_high, t0_low = call(
-        far_sent_kernel, [sent] + pair(width, block, block), [tab, a23_high, a23_low, dinv, t_0], micros=2
+        far_sent_kernel, [sent] + pair(width, block, block), [tab, m_high, m_low, t_0], micros=2
     )
     got_far_1 = exchanged(far_1, 1)
 

time: 59.8 us -> 59.2 us (0.990)
  starting transfers between devices: 26.4 us -> 29 us
  waiting for transfers between devices: 12.3 us -> 10.4 us
  Pallas kernels: 20.6 us -> 19.4 us
    ppermute x10, starting transfers between devices: 26.4 us -> 29 us  [exchanged(): return lax.ppermute(value, AXES, pairs)]
    ppermute x10, waiting for transfers between devices: 12.3 us -> 10.4 us  [exchanged(): return lax.ppermute(value, AXES, pairs)]
    pallas_call x16, Pallas kernels: 20.6 us -> 19.4 us  [call(): pl.pallas_call(body, out_shape=outs, in_specs=specs(ins, in_hbm), out_spe...]
where the time goes in v3:
time: 59.2 us; the launch traced here: 59.1 us
  starting transfers between devices  29 us (49%)
  Pallas kernels  19.4 us (33%)
  waiting for transfers between devices  10.4 us (18%)
    ppermute x10, starting transfers between devices, exchanged(): return lax.ppermute(value, AXES, pairs)  29 us
    pallas_call x16, Pallas kernels, call(): pl.pallas_call(body, out_shape=outs, in_specs=specs(ins, in_hbm), out_spe...  19.4 us
    ppermute x10, waiting for transfers between devices, exchanged(): return lax.ppermute(value, AXES, pairs)  10.4 us
  transfers between devices with their start and end apart: 10, of which 4 were waited for; matrix products, arithmetic and copies ran while one was open for 0% of the time, Pallas kernels for 18%

profile of v3, /device:TPU:0, one launch (start us, length us, event | category | flops | bytes accessed | tf_op | source)
XLA Modules:
  0.0 59.1 jit_solution(12667779207614742203)
XLA Ops:
  0.0 3.5 %shard_map.64 = (s32[96,128]{1,0:T(8,128)S(1)}, f32[4,128,128]{2,1,0:T(8,128)S(1)}, f32[4,128,128]{2,1,0:T(8,128)S(1)}, f32[8,128,128]{2,1,0:T(8,128)S(1)}, f32[...) custom-call(s32[4096]{0:T(1024)} %bitcast.5, ...), custom_call_target="tpu_custom_call" | custom-call | flops 3000000000 | bytes 1048576 | tf_op jit(solution)/shard_map/pallas_call | solution.py:472
  3.5 0.1 collective-permute-start
  3.6 6.9 %collective-permute-start.1 = (f32[4,128,128]{2,1,0:T(8,128)S(1)}, f32[4,128,128]{2,1,0:T(8,128)S(1)}, u32[]{:S(2)}, u32[]{:S(2)}) collective-permute-start(f32[4,128,128]{2,1,0:T(8,128)S(1)} %get-tuple-element.77), channel_id=1, source_target_pairs={{1,2},{2,1},{3,4},{4,3},{5,6},{6,5},{7,8},{8,7},{9,10},{10,9},{11,... | collective-permute-start | bytes 786440 | tf_op jit(solution)/shard_map/ppermute | solution.py:27
  10.5 0.0 collective-permute-start.2
  10.5 2.4 %collective-permute-start.3 = (f32[4,128,256]{2,1,0:T(8,128)S(1)}, f32[4,128,256]{2,1,0:T(8,128)S(1)}, u32[]{:S(2)}, u32[]{:S(2)}) collective-permute-start(f32[4,128,256]{2,1,0:T(8,128)S(1)} %get-tuple-element.86), channel_id=1, source_target_pairs={{1,2},{2,1},{3,4},{4,3},{5,6},{6,5},{7,8},{8,7},{9,10},{10,9},{11,... | collective-permute-start | bytes 1572872 | tf_op jit(solution)/shard_map/ppermute | solution.py:27
  12.9 0.0 collective-permute-done.t_0
  12.9 0.3 shard_map.66
  13.3 1.7 %collective-permute-done.1.t_1 = f32[4,128,128]{2,1,0:T(8,128)S(1)} collective-permute-done((f32[4,128,128]{2,1,0:T(8,128)S(1)}, f32[4,128,128]{2,1,0:T(8,128)S(1)}, u32[]{:S(2)}, u32[]{:S(2)}) %collective-permute-start.1) | collective-permute-done | bytes 262176 | tf_op jit(solution)/shard_map/ppermute | solution.py:27
  14.9 0.8 %shard_map.67 = (f32[4,2,128,128]{3,2,1,0:T(8,128)S(1)}, f32[8,2,128,128]{3,2,1,0:T(8,128)S(1)}) custom-call(s32[96,128]{1,0:T(8,128)S(1)} %get-tuple-element.56.tab, bf16[2,8,128,128]{3,2,1,0:T(8,128)(2,1)S(1)} %get-tuple-element.70.a_high, bf16[2,8,128,128]{3,2,1,0:T(8,128)(2,1)S(1)} %get-tuple-element.71.a_low, f32[8,128,128]{2,1,0:T(8,128)S(1)} %copy-done.2, ...), custom_call_target="tpu_custom_call" | custom-call | flops 1000000000 | bytes 1048576 | tf_op jit(solution)/shard_map/pallas_call | solution.py:472
  15.7 0.1 collective-permute-start.4
  15.8 0.8 %shard_map.71 = (f32[8,128,256]{2,1,0:T(8,128)S(1)}, bf16[4,128,128]{2,1,0:T(8,128)(2,1)S(1)}, bf16[4,128,128]{2,1,0:T(8,128)(2,1)S(1)}) custom-call(s32[96,128]{1,0:T(8,128)S(1)} %get-tuple-element.56.tab, bf16[8,128,256]{2,1,0:T(8,128)(2,1)S(1)} %get-tuple-element.68.a01_high, bf16[8,128,256]{2,1,0:T(8,128)(2,1)S(1)} %get-tuple-element.69.a01_low, ...), custom_call_target="tpu_custom_call" | custom-call | flops 1000000000 | bytes 1048576 | tf_op jit(solution)/shard_map/pallas_call | solution.py:472
  16.6 6.1 %collective-permute-start.5 = (f32[4,2,128,128]{3,2,1,0:T(8,128)S(1)}, f32[4,2,128,128]{3,2,1,0:T(8,128)S(1)}, u32[]{:S(2)}, u32[]{:S(2)}) collective-permute-start(f32[4,2,128,128]{3,2,1,0:T(8,128)S(1)} %get-tuple-element.78.far_1), channel_id=1, source_target_pairs={{1,2},{2,1},{3,4},{4,3},{5,6},{6,5},{7,8},{8,7},{9,10},{10,9},{11,... | collective-permute-start | bytes 1572872 | tf_op jit(solution)/shard_map/ppermute | solution.py:27
  22.7 0.0 collective-permute-done.2.near_0
  22.7 2.2 %shard_map.68 = (bf16[256,1024]{1,0:T(8,128)(2,1)S(1)}, bf16[256,1024]{1,0:T(8,128)(2,1)S(1)}, f32[8,128,256]{2,1,0:T(8,128)S(1)}, bf16[1024,256]{1,0:T(8,128)(2...) custom-call(s32[96,128]{1,0:T(8,128)S(1)} %get-tuple-element.56.tab, ...), custom_call_target="tpu_custom_call" | custom-call | flops 2000000000 | bytes 1048576 | tf_op jit(solution)/shard_map/pallas_call | solution.py:472
  24.9 0.0 collective-permute-done.3.near_1
  24.9 1.0 %shard_map.69 = (bf16[1024,256]{1,0:T(8,128)(2,1)S(1)}, bf16[1024,256]{1,0:T(8,128)(2,1)S(1)}, f32[256,256]{1,0:T(8,128)S(1)}) custom-call(s32[96,128]{1,0:T(8,128)S(1)} %get-tuple-element.56.tab, bf16[2,8,128,128]{3,2,1,0:T(8,128)(2,1)S(1)} %get-tuple-element.70.a_high, bf16[2,8,128,128]{3,2,1,0:T(8,128)(2,1)S(1)} %get-tuple-element.71.a_low, ...), custom_call_target="tpu_custom_call" | custom-call | flops 2000000000 | bytes 1048576 | tf_op jit(solution)/shard_map/pallas_call | solution.py:472
  25.9 0.0 collective-permute-done.4.far_0
  25.9 1.1 %shard_map.70 = (f32[8,128,256]{2,1,0:T(8,128)S(1)}, bf16[1024,256]{1,0:T(8,128)(2,1)S(1)}, bf16[1024,256]{1,0:T(8,128)(2,1)S(1)}, f32[256,512]{1,0:T(8,128)S(1)}) custom-call(s32[96,128]{1,0:T(8,128)S(1)} %get-tuple-element.56.tab, bf16[2,8,128,128]{3,2,1,0:T(8,128)(2,1)S(1)} %get-tuple-element.70.a_high, ...), custom_call_target="tpu_custom_call" | custom-call | flops 1000000000 | bytes 1048576 | tf_op jit(solution)/shard_map/pallas_call | solution.py:472
  27.0 3.7 %collective-permute-done.5.far_1 = f32[4,2,128,128]{3,2,1,0:T(8,128)S(1)} collective-permute-done((f32[4,2,128,128]{3,2,1,0:T(8,128)S(1)}, f32[4,2,128,128]{3,2,1,0:T(8,128)S(1)}, u32[]{:S(2)}, u32[]{:S(2)}) %collective-permute-start.5) | collective-permute-done | bytes 524320 | tf_op jit(solution)/shard_map/ppermute | solution.py:27
  30.7 1.7 %shard_map.73 = (bf16[1024,256]{1,0:T(8,128)(2,1)S(1)}, bf16[1024,256]{1,0:T(8,128)(2,1)S(1)}, bf16[1024,256]{1,0:T(8,128)(2,1)S(1)}, bf16[1024,256]{1,0:T(8,128)(2,1)S(1)}, f32[256,512]{1,0:T(8,128)S(1)}) custom-call(s32[96,128]{1,0:T(8,128)S(1)} %get-tuple-element.56.tab, bf16[2,8,128,128]{3,2,1,0:T(8,128)(2,1)S(1)} %get-tuple-element.70.a_high, ...), custom_call_target="tpu_custom_call" | custom-call | flops 2000000000 | bytes 1048576 | tf_op jit(solution)/shard_map/pallas_call | solution.py:472
  32.4 2.5 %shard_map.76 = f32[256,1280]{1,0:T(8,128)S(1)} custom-call(s32[96,128]{1,0:T(8,128)S(1)} %get-tuple-element.56.tab, f32[8,2,128,128]{3,2,1,0:T(8,128)S(1)} %get-tuple-element.79.far, bf16[1024,256]{1,0:T(8,128)(2,1)S(1)} %get-tuple-element.81.refs_0_, bf16[1024,256]{1,0:T(8,128)(2,1)S(1)} %get-tuple-element.82.refs_1_, ...), custom_call_target="tpu_custom_call" | custom-call | flops 2000000000 | bytes 1048576 | tf_op jit(solution)/shard_map/pallas_call | solution.py:472
  34.9 0.1 collective-permute-start.6
  35.0 6.1 %collective-permute-start.9 = (f32[256,512]{1,0:T(8,128)S(1)}, f32[256,512]{1,0:T(8,128)S(1)}, u32[]{:S(2)}, u32[]{:S(2)}) collective-permute-start(f32[256,512]{1,0:T(8,128)S(1)} %get-tuple-element.106), channel_id=1, source_target_pairs={{1,2},{2,1},{3,4},{4,3},{5,6},{6,5},{7,8},{8,7},{9,10},{10,9},{11,... | collective-permute-start | bytes 1572872 | tf_op jit(solution)/shard_map/ppermute | solution.py:27
  41.1 1.1 %collective-permute-start.8 = (f32[256,512]{1,0:T(8,128)S(1)}, f32[256,512]{1,0:T(8,128)S(1)}, u32[]{:S(2)}, u32[]{:S(2)}) collective-permute-start(f32[256,512]{1,0:T(8,128)S(1)} %get-tuple-element.105), channel_id=1, source_target_pairs={{1,2},{2,1},{3,4},{4,3},{5,6},{6,5},{7,8},{8,7},{9,10},{10,9},{11,... | collective-permute-start | bytes 1572872 | tf_op jit(solution)/shard_map/ppermute | solution.py:27
  42.2 6.1 %collective-permute-start.7 = (f32[256,256]{1,0:T(8,128)S(1)}, f32[256,256]{1,0:T(8,128)S(1)}, u32[]{:S(2)}, u32[]{:S(2)}) collective-permute-start(f32[256,256]{1,0:T(8,128)S(1)} %get-tuple-element.104), channel_id=1, source_target_pairs={{1,2},{2,1},{3,4},{4,3},{5,6},{6,5},{7,8},{8,7},{9,10},{10,9},{11,... | collective-permute-start | bytes 786440 | tf_op jit(solution)/shard_map/ppermute | solution.py:27
  48.3 2.3 %shard_map.75.own = f32[256,1280]{1,0:T(8,128)S(1)} custom-call(f32[8,128,256]{2,1,0:T(8,128)S(1)} %get-tuple-element.67.own, bf16[1024,256]{1,0:T(8,128)(2,1)S(1)} %get-tuple-element.81.refs_0_, bf16[1024,256]{1,0:T(8,128)(2,1)S(1)} %get-tuple-element.82.refs_1_, bf16[1024,256]{1,0:T(8,128)(2,1)S(1)} %get-tuple-element.87.refs_2_, ...), custom_call_target="tpu_custom_call", output_to_operand_aliasing={{}: (11, {})} | custom-call | flops 2000000000 | bytes 1048576 | tf_op jit(solution)/shard_map/pallas_call | solution.py:472
  50.6 0.0 collective-permute-done.9.refs_0_
  50.6 1.1 %shard_map.77.refs_2_ = f32[2,14,128,128]{3,2,1,0:T(8,128)} custom-call(f32[2,128,128]{2,1,0:T(8,128)S(1)} %copy-done.1, f32[256,1280]{1,0:T(8,128)S(1)} %shard_map.75.own, f32[256,512]{1,0:T(8,128)S(1)} %collective-permute-done.9.refs_0_), custom_call_target="tpu_custom_call" | custom-call | flops 1000000000 | bytes 1048576 | tf_op jit(solution)/shard_map/pallas_call | solution.py:472
  51.7 3.5 %collective-permute-done.8.refs_1_ = f32[256,512]{1,0:T(8,128)S(1)} collective-permute-done((f32[256,512]{1,0:T(8,128)S(1)}, f32[256,512]{1,0:T(8,128)S(1)}, u32[]{:S(2)}, u32[]{:S(2)}) %collective-permute-start.8) | collective-permute-done | bytes 524320 | tf_op jit(solution)/shard_map/ppermute | solution.py:27
  55.2 1.3 %shard_map.78.refs_2_ = f32[2,14,128,128]{3,2,1,0:T(8,128)} custom-call(f32[2,128,128]{2,1,0:T(8,128)S(1)} %copy-done.1, f32[256,1280]{1,0:T(8,128)S(1)} %shard_map.75.own, f32[256,1280]{1,0:T(8,128)S(1)} %collective-permute-done.6.refs_0_, f32[256,512]{1,0:T(8,128)S(1)} %collective-permute-done.8.refs_1_, ...), custom_call_target="tpu_custom_call", output_to_operand_aliasing={{}: (4, {})} | custom-call | flops 1000000000 | bytes 1048576 | tf_op jit(solution)/shard_map/pallas_call | solution.py:472
  56.4 1.5 %collective-permute-done.7.refs_1_ = f32[256,256]{1,0:T(8,128)S(1)} collective-permute-done((f32[256,256]{1,0:T(8,128)S(1)}, f32[256,256]{1,0:T(8,128)S(1)}, u32[]{:S(2)}, u32[]{:S(2)}) %collective-permute-start.7) | collective-permute-done | bytes 262176 | tf_op jit(solution)/shard_map/ppermute | solution.py:27
  58.0 1.0 %shard_map.79 = f32[2,14,128,128]{3,2,1,0:T(8,128)} custom-call(f32[2,128,128]{2,1,0:T(8,128)S(1)} %copy-done.1, f32[256,1280]{1,0:T(8,128)S(1)} %shard_map.75.own, f32[256,1280]{1,0:T(8,128)S(1)} %collective-permute-done.6.refs_0_, f32[256,256]{1,0:T(8,128)S(1)} %collective-permute-done.7.refs_1_, ...), custom_call_target="tpu_custom_call", output_to_operand_aliasing={{}: (4, {})} | custom-call | flops 1000000000 | bytes 1048576 | tf_op jit(solution)/shard_map/pallas_call | solution.py:472
  (10 shorter events, 0.0 us)
Async XLA Ops:
  0.0 10.5 %copy-start = (f32[8,4,128,128]{3,2,1,0:T(8,128)S(1)}, f32[8,4,128,128]{3,2,1,0:T(8,128)}, u32[]{:S(2)}) copy-start(f32[8,4,128,128]{3,2,1,0:T(8,128)} %a.1) | copy-start | bytes 6291460
  0.0 10.5 %copy-start.2 = (f32[8,128,128]{2,1,0:T(8,128)S(1)}, f32[8,128,128]{2,1,0:T(8,128)}, u32[]{:S(2)}) copy-start(f32[8,128,128]{2,1,0:T(8,128)} %dinv.3) | copy-start | bytes 1572868
  3.5 9.4 %collective-permute-start = (f32[4,128,128]{2,1,0:T(8,128)S(1)}, f32[4,128,128]{2,1,0:T(8,128)S(1)}, u32[]{:S(2)}, u32[]{:S(2)}) collective-permute-start(f32[4,128,128]{2,1,0:T(8,128)S(1)} %get-tuple-element.74), channel_id=1, source_target_pairs={{0,1},{1,0},{2,3},{3,2},{4,5},{5,4},{6,7},{7,6},{8,9},{9,8},{10,11... | collective-permute-start | bytes 786440 | tf_op jit(solution)/shard_map/ppermute | solution.py:27
  3.6 11.3 %collective-permute-start.1 = (f32[4,128,128]{2,1,0:T(8,128)S(1)}, f32[4,128,128]{2,1,0:T(8,128)S(1)}, u32[]{:S(2)}, u32[]{:S(2)}) collective-permute-start(f32[4,128,128]{2,1,0:T(8,128)S(1)} %get-tuple-element.77), channel_id=1, source_target_pairs={{1,2},{2,1},{3,4},{4,3},{5,6},{6,5},{7,8},{8,7},{9,10},{10,9},{11,... | collective-permute-start | bytes 786440 | tf_op jit(solution)/shard_map/ppermute | solution.py:27
  10.5 12.2 %collective-permute-start.2 = (f32[4,128,256]{2,1,0:T(8,128)S(1)}, f32[4,128,256]{2,1,0:T(8,128)S(1)}, u32[]{:S(2)}, u32[]{:S(2)}) collective-permute-start(f32[4,128,256]{2,1,0:T(8,128)S(1)} %get-tuple-element.80), channel_id=1, source_target_pairs={{0,1},{1,0},{2,3},{3,2},{4,5},{5,4},{6,7},{7,6},{8,9},{9,8},{10,11... | collective-permute-start | bytes 1572872 | tf_op jit(solution)/shard_map/ppermute | solution.py:27
  10.5 14.4 %collective-permute-start.3 = (f32[4,128,256]{2,1,0:T(8,128)S(1)}, f32[4,128,256]{2,1,0:T(8,128)S(1)}, u32[]{:S(2)}, u32[]{:S(2)}) collective-permute-start(f32[4,128,256]{2,1,0:T(8,128)S(1)} %get-tuple-element.86), channel_id=1, source_target_pairs={{1,2},{2,1},{3,4},{4,3},{5,6},{6,5},{7,8},{8,7},{9,10},{10,9},{11,... | collective-permute-start | bytes 1572872 | tf_op jit(solution)/shard_map/ppermute | solution.py:27
  15.7 10.2 %collective-permute-start.4 = (f32[4,2,128,128]{3,2,1,0:T(8,128)S(1)}, f32[4,2,128,128]{3,2,1,0:T(8,128)S(1)}, u32[]{:S(2)}, u32[]{:S(2)}) collective-permute-start(f32[4,2,128,128]{3,2,1,0:T(8,128)S(1)} %get-tuple-element.89), channel_id=1, source_target_pairs={{0,1},{1,0},{2,3},{3,2},{4,5},{5,4},{6,7},{7,6},{8,9},{9,8},{10,11... | collective-permute-start | bytes 1572872 | tf_op jit(solution)/shard_map/ppermute | solution.py:27
  16.6 14.1 %collective-permute-start.5 = (f32[4,2,128,128]{3,2,1,0:T(8,128)S(1)}, f32[4,2,128,128]{3,2,1,0:T(8,128)S(1)}, u32[]{:S(2)}, u32[]{:S(2)}) collective-permute-start(f32[4,2,128,128]{3,2,1,0:T(8,128)S(1)} %get-tuple-element.78.far_1), channel_id=1, source_target_pairs={{1,2},{2,1},{3,4},{4,3},{5,6},{6,5},{7,8},{8,7},{9,10},{10,9},{11,... | collective-permute-start | bytes 1572872 | tf_op jit(solution)/shard_map/ppermute | solution.py:27
  34.9 20.3 %collective-permute-start.6 = (f32[256,1280]{1,0:T(8,128)S(1)}, f32[256,1280]{1,0:T(8,128)S(1)}, u32[]{:S(2)}, u32[]{:S(2)}) collective-permute-start(f32[256,1280]{1,0:T(8,128)S(1)} %shard_map.76), channel_id=1, source_target_pairs={{0,1},{1,0},{2,3},{3,2},{4,5},{5,4},{6,7},{7,6},{8,9},{9,8},{10,11... | collective-permute-start | bytes 3932168 | tf_op jit(solution)/shard_map/ppermute | solution.py:27
  35.0 15.6 %collective-permute-start.9 = (f32[256,512]{1,0:T(8,128)S(1)}, f32[256,512]{1,0:T(8,128)S(1)}, u32[]{:S(2)}, u32[]{:S(2)}) collective-permute-start(f32[256,512]{1,0:T(8,128)S(1)} %get-tuple-element.106), channel_id=1, source_target_pairs={{1,2},{2,1},{3,4},{4,3},{5,6},{6,5},{7,8},{8,7},{9,10},{10,9},{11,... | collective-permute-start | bytes 1572872 | tf_op jit(solution)/shard_map/ppermute | solution.py:27
  41.1 14.0 %collective-permute-start.8 = (f32[256,512]{1,0:T(8,128)S(1)}, f32[256,512]{1,0:T(8,128)S(1)}, u32[]{:S(2)}, u32[]{:S(2)}) collective-permute-start(f32[256,512]{1,0:T(8,128)S(1)} %get-tuple-element.105), channel_id=1, source_target_pairs={{1,2},{2,1},{3,4},{4,3},{5,6},{6,5},{7,8},{8,7},{9,10},{10,9},{11,... | collective-permute-start | bytes 1572872 | tf_op jit(solution)/shard_map/ppermute | solution.py:27
  42.2 15.7 %collective-permute-start.7 = (f32[256,256]{1,0:T(8,128)S(1)}, f32[256,256]{1,0:T(8,128)S(1)}, u32[]{:S(2)}, u32[]{:S(2)}) collective-permute-start(f32[256,256]{1,0:T(8,128)S(1)} %get-tuple-element.104), channel_id=1, source_target_pairs={{1,2},{2,1},{3,4},{4,3},{5,6},{6,5},{7,8},{8,7},{9,10},{10,9},{11,... | collective-permute-start | bytes 786440 | tf_op jit(solution)/shard_map/ppermute | solution.py:27
  48.3 2.3 %copy-start.1 = (f32[2,128,128]{2,1,0:T(8,128)S(1)}, f32[2,128,128]{2,1,0:T(8,128)}, u32[]{:S(2)}) copy-start(f32[2,128,128]{2,1,0:T(8,128)} %inverse.5) | copy-start | bytes 393220

commit v4 on v3

--- a/solution.py
+++ b/solution.py
@@ -277,48 +277,48 @@
 
 def mid_kernel(
     tab, a01_high, a01_low, a_high, a_low, far, near_0,
-    trans_high, trans_low, part, ap_high, ap_low, group,
+    trans_high, trans_low, away_high, away_low, ap_high, ap_low, group,
     far_high, far_low, p_high, p_low,
 ):
     rows, block = far.shape[0], far.shape[2]
     side = pair_side()
     split_rows(near_0, p_high, p_low)
     for u in range(rows):
-        for which in (BELOW, ABOVE):
+        for which, high_ref, low_ref in ((side, far_high, far_low), (1 - side, away_high, away_low)):
             label = entry(tab, OWN_LAB + 4 * u + 2 + which)
             high, low = split(far[u, which])
-            far_high[which, u] = two_columns(high, label)
-            far_low[which, u] = two_columns(low, label)
-
-    def mine(u, which):
+            high_ref[u] = two_columns(high, label)
+            low_ref[u] = two_columns(low, label)
+
+    def mine(u):
         near = entry(tab, NEAR + u)
-        return dot3(a01_high[u], a01_low[u], wide(far_high.at[which], u, near), wide(far_low.at[which], u, near))
+        return dot3(a01_high[u], a01_low[u], wide(far_high, u, near), wide(far_low, u, near))
 
     totals = []
     for u in range(rows):
         pos = entry(tab, POS2 + 8 * side + u)
-        totals.append(mine(u, side) + dot3k(a_high[side, u], a_low[side, u], p_high[pos], p_low[pos]))
+        totals.append(mine(u) + dot3k(a_high[side, u], a_low[side, u], p_high[pos], p_low[pos]))
     for u in range(rows):
         place = slice(u * block, (u + 1) * block)
         ap_high[place], ap_low[place] = split(totals[u])
     turn(tab, far, 1 - side, trans_high, trans_low)
-    for u in range(rows):
-        part[u] = mine(u, 1 - side)
     group[...] = coarse_group(trans_high, trans_low, ap_high, ap_low)
 
 
 def first_kernel(
-    tab, a_high, a_low, part, trans_high, trans_low, near_1,
+    tab, a01_high, a01_low, a_high, a_low, away_high, away_low, trans_high, trans_low, near_1,
     ap_high, ap_low, out_1,
     p_high, p_low,
 ):
-    rows, block = part.shape[0], part.shape[1]
+    rows, block = away_high.shape[0], away_high.shape[1]
     side = 1 - pair_side()
     split_rows(near_1, p_high, p_low)
     totals = []
     for u in range(rows):
         pos = entry(tab, POS2 + 8 * side + u)
-        totals.append(part[u] + dot3k(a_high[side, u], a_low[side, u], p_high[pos], p_low[pos]))
+        near = entry(tab, NEAR + u)
+        mine = dot3(a01_high[u], a01_low[u], wide(away_high, u, near), wide(away_low, u, near))
+        totals.append(mine + dot3k(a_high[side, u], a_low[side, u], p_high[pos], p_low[pos]))
     for u in range(rows):
         place = slice(u * block, (u + 1) * block)
         ap_high[place], ap_low[place] = split(totals[u])
@@ -541,11 +541,11 @@
         micros=1,
     )
     far_0, far_1 = exchanged(far_0, 0), got_far_1
-    out_high, out_low, part, ap_e1_high, ap_e1_low, group = call(
+    out_high, out_low, away_high, away_low, ap_e1_high, ap_e1_low, group = call(
         mid_kernel,
-        pair(half, deep) + [full(rows, block, half)] + pair(deep, half) + [full(half, half)],
+        pair(half, deep) + pair(rows, block, half) + pair(deep, half) + [full(half, half)],
         [tab, a01_high, a01_low, a23_high, a23_low, far, near_0],
-        two(2, rows, block, half) + two(width, block, half),
+        two(rows, block, half) + two(width, block, half),
         micros=2,
     )
     part_own, ap_e2_high, ap_e2_low, part_1 = call(
@@ -568,7 +568,7 @@
     ap_o1_high, ap_o1_low, part_3 = call(
         first_kernel,
         pair(deep, half) + [full(half, half)],
-        [tab, a23_high, a23_low, part, out_high, out_low, near_1],
+        [tab, a01_high, a01_low, a23_high, a23_low, away_high, away_low, out_high, out_low, near_1],
         two(width, block, half),
         micros=2,
     )

time: 59.2 us -> 59.2 us (level)
  transfers between devices with their start and end apart: 10 -> 10, of which waited for: 4 -> 5; matrix products, arithmetic and copies ran while one was open for 0% -> 0% of each run, Pallas kernels for 18% -> 18%
where the time goes in v4:
time: 59.2 us; the launch traced here: 59.1 us
  starting transfers between devices  29 us (49%)
  Pallas kernels  19.4 us (33%)
  waiting for transfers between devices  10.3 us (17%)
    ppermute x10, starting transfers between devices, exchanged(): return lax.ppermute(value, AXES, pairs)  29 us
    pallas_call x16, Pallas kernels, call(): pl.pallas_call(body, out_shape=outs, in_specs=specs(ins, in_hbm), out_spe...  19.4 us
    ppermute x10, waiting for transfers between devices, exchanged(): return lax.ppermute(value, AXES, pairs)  10.3 us
  transfers between devices with their start and end apart: 10, of which 5 were waited for; matrix products, arithmetic and copies ran while one was open for 0% of the time, Pallas kernels for 18%

profile of v4, /device:TPU:0, one launch (start us, length us, event | category | flops | bytes accessed | tf_op | source)
XLA Modules:
  0.0 59.1 jit_solution(16258899123469214117)
XLA Ops:
  0.0 3.5 %shard_map.64 = (s32[96,128]{1,0:T(8,128)S(1)}, f32[4,128,128]{2,1,0:T(8,128)S(1)}, f32[4,128,128]{2,1,0:T(8,128)S(1)}, f32[8,128,128]{2,1,0:T(8,128)S(1)}, f32[...) custom-call(s32[4096]{0:T(1024)} %bitcast.5, ...), custom_call_target="tpu_custom_call" | custom-call | flops 3000000000 | bytes 1048576 | tf_op jit(solution)/shard_map/pallas_call | solution.py:472
  3.5 0.1 collective-permute-start
  3.6 6.9 %collective-permute-start.1 = (f32[4,128,128]{2,1,0:T(8,128)S(1)}, f32[4,128,128]{2,1,0:T(8,128)S(1)}, u32[]{:S(2)}, u32[]{:S(2)}) collective-permute-start(f32[4,128,128]{2,1,0:T(8,128)S(1)} %get-tuple-element.78), channel_id=1, source_target_pairs={{1,2},{2,1},{3,4},{4,3},{5,6},{6,5},{7,8},{8,7},{9,10},{10,9},{11,... | collective-permute-start | bytes 786440 | tf_op jit(solution)/shard_map/ppermute | solution.py:27
  10.5 0.0 collective-permute-start.2
  10.5 2.4 %collective-permute-start.3 = (f32[4,128,256]{2,1,0:T(8,128)S(1)}, f32[4,128,256]{2,1,0:T(8,128)S(1)}, u32[]{:S(2)}, u32[]{:S(2)}) collective-permute-start(f32[4,128,256]{2,1,0:T(8,128)S(1)} %get-tuple-element.88), channel_id=1, source_target_pairs={{1,2},{2,1},{3,4},{4,3},{5,6},{6,5},{7,8},{8,7},{9,10},{10,9},{11,... | collective-permute-start | bytes 1572872 | tf_op jit(solution)/shard_map/ppermute | solution.py:27
  12.9 0.0 collective-permute-done.t_0
  12.9 0.3 shard_map.66
  13.3 1.7 %collective-permute-done.1.t_1 = f32[4,128,128]{2,1,0:T(8,128)S(1)} collective-permute-done((f32[4,128,128]{2,1,0:T(8,128)S(1)}, f32[4,128,128]{2,1,0:T(8,128)S(1)}, u32[]{:S(2)}, u32[]{:S(2)}) %collective-permute-start.1) | collective-permute-done | bytes 262176 | tf_op jit(solution)/shard_map/ppermute | solution.py:27
  14.9 0.8 %shard_map.67 = (f32[4,2,128,128]{3,2,1,0:T(8,128)S(1)}, f32[8,2,128,128]{3,2,1,0:T(8,128)S(1)}) custom-call(s32[96,128]{1,0:T(8,128)S(1)} %get-tuple-element.57.tab, bf16[2,8,128,128]{3,2,1,0:T(8,128)(2,1)S(1)} %get-tuple-element.71.a_high, bf16[2,8,128,128]{3,2,1,0:T(8,128)(2,1)S(1)} %get-tuple-element.72.a_low, f32[8,128,128]{2,1,0:T(8,128)S(1)} %copy-done.2, ...), custom_call_target="tpu_custom_call" | custom-call | flops 1000000000 | bytes 1048576 | tf_op jit(solution)/shard_map/pallas_call | solution.py:472
  15.7 0.1 collective-permute-start.4
  15.8 0.8 %shard_map.71 = (f32[8,128,256]{2,1,0:T(8,128)S(1)}, bf16[4,128,128]{2,1,0:T(8,128)(2,1)S(1)}, bf16[4,128,128]{2,1,0:T(8,128)(2,1)S(1)}) custom-call(s32[96,128]{1,0:T(8,128)S(1)} %get-tuple-element.57.tab, bf16[8,128,256]{2,1,0:T(8,128)(2,1)S(1)} %get-tuple-element.69.a01_high, bf16[8,128,256]{2,1,0:T(8,128)(2,1)S(1)} %get-tuple-element.70.a01_low, ...), custom_call_target="tpu_custom_call" | custom-call | flops 1000000000 | bytes 1048576 | tf_op jit(solution)/shard_map/pallas_call | solution.py:472
  16.6 6.1 %collective-permute-start.5 = (f32[4,2,128,128]{3,2,1,0:T(8,128)S(1)}, f32[4,2,128,128]{3,2,1,0:T(8,128)S(1)}, u32[]{:S(2)}, u32[]{:S(2)}) collective-permute-start(f32[4,2,128,128]{3,2,1,0:T(8,128)S(1)} %get-tuple-element.79.far_1), channel_id=1, source_target_pairs={{1,2},{2,1},{3,4},{4,3},{5,6},{6,5},{7,8},{8,7},{9,10},{10,9},{11,... | collective-permute-start | bytes 1572872 | tf_op jit(solution)/shard_map/ppermute | solution.py:27
  22.7 0.0 collective-permute-done.2.near_0
  22.7 1.8 %shard_map.68 = (bf16[256,1024]{1,0:T(8,128)(2,1)S(1)}, bf16[256,1024]{1,0:T(8,128)(2,1)S(1)}, bf16[8,128,256]{2,1,0:T(8,128)(2,1)S(1)}, bf16[8,128,256]{2,1,0:T...) custom-call(s32[96,128]{1,0:T(8,128)S(1)} %get-tuple-element.57.tab, ...), custom_call_target="tpu_custom_call" | custom-call | flops 2000000000 | bytes 1048576 | tf_op jit(solution)/shard_map/pallas_call | solution.py:472
  24.5 0.1 collective-permute-done.3.near_1
  24.6 1.4 %shard_map.69 = (bf16[1024,256]{1,0:T(8,128)(2,1)S(1)}, bf16[1024,256]{1,0:T(8,128)(2,1)S(1)}, f32[256,256]{1,0:T(8,128)S(1)}) custom-call(s32[96,128]{1,0:T(8,128)S(1)} %get-tuple-element.57.tab, bf16[8,128,256]{2,1,0:T(8,128)(2,1)S(1)} %get-tuple-element.69.a01_high, bf16[8,128,256]{2,1,0:T(8,128)(2,1)S(1)} %get-tuple-element.70.a01_low, ...), custom_call_target="tpu_custom_call" | custom-call | flops 2000000000 | bytes 1048576 | tf_op jit(solution)/shard_map/pallas_call | solution.py:472
  26.0 0.0 collective-permute-done.4.far_0
  26.0 1.1 %shard_map.70 = (f32[8,128,256]{2,1,0:T(8,128)S(1)}, bf16[1024,256]{1,0:T(8,128)(2,1)S(1)}, bf16[1024,256]{1,0:T(8,128)(2,1)S(1)}, f32[256,512]{1,0:T(8,128)S(1)}) custom-call(s32[96,128]{1,0:T(8,128)S(1)} %get-tuple-element.57.tab, bf16[2,8,128,128]{3,2,1,0:T(8,128)(2,1)S(1)} %get-tuple-element.71.a_high, ...), custom_call_target="tpu_custom_call" | custom-call | flops 1000000000 | bytes 1048576 | tf_op jit(solution)/shard_map/pallas_call | solution.py:472
  27.1 3.6 %collective-permute-done.5.far_1 = f32[4,2,128,128]{3,2,1,0:T(8,128)S(1)} collective-permute-done((f32[4,2,128,128]{3,2,1,0:T(8,128)S(1)}, f32[4,2,128,128]{3,2,1,0:T(8,128)S(1)}, u32[]{:S(2)}, u32[]{:S(2)}) %collective-permute-start.5) | collective-permute-done | bytes 524320 | tf_op jit(solution)/shard_map/ppermute | solution.py:27
  30.7 1.7 %shard_map.73 = (bf16[1024,256]{1,0:T(8,128)(2,1)S(1)}, bf16[1024,256]{1,0:T(8,128)(2,1)S(1)}, bf16[1024,256]{1,0:T(8,128)(2,1)S(1)}, bf16[1024,256]{1,0:T(8,128)(2,1)S(1)}, f32[256,512]{1,0:T(8,128)S(1)}) custom-call(s32[96,128]{1,0:T(8,128)S(1)} %get-tuple-element.57.tab, bf16[2,8,128,128]{3,2,1,0:T(8,128)(2,1)S(1)} %get-tuple-element.71.a_high, ...), custom_call_target="tpu_custom_call" | custom-call | flops 2000000000 | bytes 1048576 | tf_op jit(solution)/shard_map/pallas_call | solution.py:472
  32.4 2.5 %shard_map.76 = f32[256,1280]{1,0:T(8,128)S(1)} custom-call(s32[96,128]{1,0:T(8,128)S(1)} %get-tuple-element.57.tab, f32[8,2,128,128]{3,2,1,0:T(8,128)S(1)} %get-tuple-element.80.far, bf16[1024,256]{1,0:T(8,128)(2,1)S(1)} %get-tuple-element.82.refs_0_, bf16[1024,256]{1,0:T(8,128)(2,1)S(1)} %get-tuple-element.83.refs_1_, ...), custom_call_target="tpu_custom_call" | custom-call | flops 2000000000 | bytes 1048576 | tf_op jit(solution)/shard_map/pallas_call | solution.py:472
  34.9 0.1 collective-permute-start.6
  35.0 6.1 %collective-permute-start.9 = (f32[256,512]{1,0:T(8,128)S(1)}, f32[256,512]{1,0:T(8,128)S(1)}, u32[]{:S(2)}, u32[]{:S(2)}) collective-permute-start(f32[256,512]{1,0:T(8,128)S(1)} %get-tuple-element.108), channel_id=1, source_target_pairs={{1,2},{2,1},{3,4},{4,3},{5,6},{6,5},{7,8},{8,7},{9,10},{10,9},{11,... | collective-permute-start | bytes 1572872 | tf_op jit(solution)/shard_map/ppermute | solution.py:27
  41.1 1.1 %collective-permute-start.8 = (f32[256,512]{1,0:T(8,128)S(1)}, f32[256,512]{1,0:T(8,128)S(1)}, u32[]{:S(2)}, u32[]{:S(2)}) collective-permute-start(f32[256,512]{1,0:T(8,128)S(1)} %get-tuple-element.107), channel_id=1, source_target_pairs={{1,2},{2,1},{3,4},{4,3},{5,6},{6,5},{7,8},{8,7},{9,10},{10,9},{11,... | collective-permute-start | bytes 1572872 | tf_op jit(solution)/shard_map/ppermute | solution.py:27
  42.2 6.1 %collective-permute-start.7 = (f32[256,256]{1,0:T(8,128)S(1)}, f32[256,256]{1,0:T(8,128)S(1)}, u32[]{:S(2)}, u32[]{:S(2)}) collective-permute-start(f32[256,256]{1,0:T(8,128)S(1)} %get-tuple-element.106), channel_id=1, source_target_pairs={{1,2},{2,1},{3,4},{4,3},{5,6},{6,5},{7,8},{8,7},{9,10},{10,9},{11,... | collective-permute-start | bytes 786440 | tf_op jit(solution)/shard_map/ppermute | solution.py:27
  48.3 2.3 %shard_map.75.own = f32[256,1280]{1,0:T(8,128)S(1)} custom-call(f32[8,128,256]{2,1,0:T(8,128)S(1)} %get-tuple-element.68.own, bf16[1024,256]{1,0:T(8,128)(2,1)S(1)} %get-tuple-element.82.refs_0_, bf16[1024,256]{1,0:T(8,128)(2,1)S(1)} %get-tuple-element.83.refs_1_, bf16[1024,256]{1,0:T(8,128)(2,1)S(1)} %get-tuple-element.89.refs_2_, ...), custom_call_target="tpu_custom_call", output_to_operand_aliasing={{}: (11, {})} | custom-call | flops 2000000000 | bytes 1048576 | tf_op jit(solution)/shard_map/pallas_call | solution.py:472
  50.6 0.0 collective-permute-done.9.refs_0_
  50.6 1.1 %shard_map.77.refs_2_ = f32[2,14,128,128]{3,2,1,0:T(8,128)} custom-call(f32[2,128,128]{2,1,0:T(8,128)S(1)} %copy-done.1, f32[256,1280]{1,0:T(8,128)S(1)} %shard_map.75.own, f32[256,512]{1,0:T(8,128)S(1)} %collective-permute-done.9.refs_0_), custom_call_target="tpu_custom_call" | custom-call | flops 1000000000 | bytes 1048576 | tf_op jit(solution)/shard_map/pallas_call | solution.py:472
  51.7 3.5 %collective-permute-done.8.refs_1_ = f32[256,512]{1,0:T(8,128)S(1)} collective-permute-done((f32[256,512]{1,0:T(8,128)S(1)}, f32[256,512]{1,0:T(8,128)S(1)}, u32[]{:S(2)}, u32[]{:S(2)}) %collective-permute-start.8) | collective-permute-done | bytes 524320 | tf_op jit(solution)/shard_map/ppermute | solution.py:27
  55.2 1.3 %shard_map.78.refs_2_ = f32[2,14,128,128]{3,2,1,0:T(8,128)} custom-call(f32[2,128,128]{2,1,0:T(8,128)S(1)} %copy-done.1, f32[256,1280]{1,0:T(8,128)S(1)} %shard_map.75.own, f32[256,1280]{1,0:T(8,128)S(1)} %collective-permute-done.6.refs_0_, f32[256,512]{1,0:T(8,128)S(1)} %collective-permute-done.8.refs_1_, ...), custom_call_target="tpu_custom_call", output_to_operand_aliasing={{}: (4, {})} | custom-call | flops 1000000000 | bytes 1048576 | tf_op jit(solution)/shard_map/pallas_call | solution.py:472
  56.4 1.5 %collective-permute-done.7.refs_1_ = f32[256,256]{1,0:T(8,128)S(1)} collective-permute-done((f32[256,256]{1,0:T(8,128)S(1)}, f32[256,256]{1,0:T(8,128)S(1)}, u32[]{:S(2)}, u32[]{:S(2)}) %collective-permute-start.7) | collective-permute-done | bytes 262176 | tf_op jit(solution)/shard_map/ppermute | solution.py:27
  58.0 1.0 %shard_map.79 = f32[2,14,128,128]{3,2,1,0:T(8,128)} custom-call(f32[2,128,128]{2,1,0:T(8,128)S(1)} %copy-done.1, f32[256,1280]{1,0:T(8,128)S(1)} %shard_map.75.own, f32[256,1280]{1,0:T(8,128)S(1)} %collective-permute-done.6.refs_0_, f32[256,256]{1,0:T(8,128)S(1)} %collective-permute-done.7.refs_1_, ...), custom_call_target="tpu_custom_call", output_to_operand_aliasing={{}: (4, {})} | custom-call | flops 1000000000 | bytes 1048576 | tf_op jit(solution)/shard_map/pallas_call | solution.py:472
  (10 shorter events, 0.0 us)
Async XLA Ops:
  0.0 10.5 %copy-start = (f32[8,4,128,128]{3,2,1,0:T(8,128)S(1)}, f32[8,4,128,128]{3,2,1,0:T(8,128)}, u32[]{:S(2)}) copy-start(f32[8,4,128,128]{3,2,1,0:T(8,128)} %a.1) | copy-start | bytes 6291460
  0.0 10.5 %copy-start.2 = (f32[8,128,128]{2,1,0:T(8,128)S(1)}, f32[8,128,128]{2,1,0:T(8,128)}, u32[]{:S(2)}) copy-start(f32[8,128,128]{2,1,0:T(8,128)} %dinv.3) | copy-start | bytes 1572868
  3.5 9.4 %collective-permute-start = (f32[4,128,128]{2,1,0:T(8,128)S(1)}, f32[4,128,128]{2,1,0:T(8,128)S(1)}, u32[]{:S(2)}, u32[]{:S(2)}) collective-permute-start(f32[4,128,128]{2,1,0:T(8,128)S(1)} %get-tuple-element.75), channel_id=1, source_target_pairs={{0,1},{1,0},{2,3},{3,2},{4,5},{5,4},{6,7},{7,6},{8,9},{9,8},{10,11... | collective-permute-start | bytes 786440 | tf_op jit(solution)/shard_map/ppermute | solution.py:27
  3.6 11.3 %collective-permute-start.1 = (f32[4,128,128]{2,1,0:T(8,128)S(1)}, f32[4,128,128]{2,1,0:T(8,128)S(1)}, u32[]{:S(2)}, u32[]{:S(2)}) collective-permute-start(f32[4,128,128]{2,1,0:T(8,128)S(1)} %get-tuple-element.78), channel_id=1, source_target_pairs={{1,2},{2,1},{3,4},{4,3},{5,6},{6,5},{7,8},{8,7},{9,10},{10,9},{11,... | collective-permute-start | bytes 786440 | tf_op jit(solution)/shard_map/ppermute | solution.py:27
  10.5 12.2 %collective-permute-start.2 = (f32[4,128,256]{2,1,0:T(8,128)S(1)}, f32[4,128,256]{2,1,0:T(8,128)S(1)}, u32[]{:S(2)}, u32[]{:S(2)}) collective-permute-start(f32[4,128,256]{2,1,0:T(8,128)S(1)} %get-tuple-element.81), channel_id=1, source_target_pairs={{0,1},{1,0},{2,3},{3,2},{4,5},{5,4},{6,7},{7,6},{8,9},{9,8},{10,11... | collective-permute-start | bytes 1572872 | tf_op jit(solution)/shard_map/ppermute | solution.py:27
  10.5 14.1 %collective-permute-start.3 = (f32[4,128,256]{2,1,0:T(8,128)S(1)}, f32[4,128,256]{2,1,0:T(8,128)S(1)}, u32[]{:S(2)}, u32[]{:S(2)}) collective-permute-start(f32[4,128,256]{2,1,0:T(8,128)S(1)} %get-tuple-element.88), channel_id=1, source_target_pairs={{1,2},{2,1},{3,4},{4,3},{5,6},{6,5},{7,8},{8,7},{9,10},{10,9},{11,... | collective-permute-start | bytes 1572872 | tf_op jit(solution)/shard_map/ppermute | solution.py:27
  15.7 10.3 %collective-permute-start.4 = (f32[4,2,128,128]{3,2,1,0:T(8,128)S(1)}, f32[4,2,128,128]{3,2,1,0:T(8,128)S(1)}, u32[]{:S(2)}, u32[]{:S(2)}) collective-permute-start(f32[4,2,128,128]{3,2,1,0:T(8,128)S(1)} %get-tuple-element.91), channel_id=1, source_target_pairs={{0,1},{1,0},{2,3},{3,2},{4,5},{5,4},{6,7},{7,6},{8,9},{9,8},{10,11... | collective-permute-start | bytes 1572872 | tf_op jit(solution)/shard_map/ppermute | solution.py:27
  16.6 14.1 %collective-permute-start.5 = (f32[4,2,128,128]{3,2,1,0:T(8,128)S(1)}, f32[4,2,128,128]{3,2,1,0:T(8,128)S(1)}, u32[]{:S(2)}, u32[]{:S(2)}) collective-permute-start(f32[4,2,128,128]{3,2,1,0:T(8,128)S(1)} %get-tuple-element.79.far_1), channel_id=1, source_target_pairs={{1,2},{2,1},{3,4},{4,3},{5,6},{6,5},{7,8},{8,7},{9,10},{10,9},{11,... | collective-permute-start | bytes 1572872 | tf_op jit(solution)/shard_map/ppermute | solution.py:27
  34.9 20.3 %collective-permute-start.6 = (f32[256,1280]{1,0:T(8,128)S(1)}, f32[256,1280]{1,0:T(8,128)S(1)}, u32[]{:S(2)}, u32[]{:S(2)}) collective-permute-start(f32[256,1280]{1,0:T(8,128)S(1)} %shard_map.76), channel_id=1, source_target_pairs={{0,1},{1,0},{2,3},{3,2},{4,5},{5,4},{6,7},{7,6},{8,9},{9,8},{10,11... | collective-permute-start | bytes 3932168 | tf_op jit(solution)/shard_map/ppermute | solution.py:27
  35.0 15.6 %collective-permute-start.9 = (f32[256,512]{1,0:T(8,128)S(1)}, f32[256,512]{1,0:T(8,128)S(1)}, u32[]{:S(2)}, u32[]{:S(2)}) collective-permute-start(f32[256,512]{1,0:T(8,128)S(1)} %get-tuple-element.108), channel_id=1, source_target_pairs={{1,2},{2,1},{3,4},{4,3},{5,6},{6,5},{7,8},{8,7},{9,10},{10,9},{11,... | collective-permute-start | bytes 1572872 | tf_op jit(solution)/shard_map/ppermute | solution.py:27
  41.1 14.0 %collective-permute-start.8 = (f32[256,512]{1,0:T(8,128)S(1)}, f32[256,512]{1,0:T(8,128)S(1)}, u32[]{:S(2)}, u32[]{:S(2)}) collective-permute-start(f32[256,512]{1,0:T(8,128)S(1)} %get-tuple-element.107), channel_id=1, source_target_pairs={{1,2},{2,1},{3,4},{4,3},{5,6},{6,5},{7,8},{8,7},{9,10},{10,9},{11,... | collective-permute-start | bytes 1572872 | tf_op jit(solution)/shard_map/ppermute | solution.py:27
  42.2 15.7 %collective-permute-start.7 = (f32[256,256]{1,0:T(8,128)S(1)}, f32[256,256]{1,0:T(8,128)S(1)}, u32[]{:S(2)}, u32[]{:S(2)}) collective-permute-start(f32[256,256]{1,0:T(8,128)S(1)} %get-tuple-element.106), channel_id=1, source_target_pairs={{1,2},{2,1},{3,4},{4,3},{5,6},{6,5},{7,8},{8,7},{9,10},{10,9},{11,... | collective-permute-start | bytes 786440 | tf_op jit(solution)/shard_map/ppermute | solution.py:27
  48.3 2.3 %copy-start.1 = (f32[2,128,128]{2,1,0:T(8,128)S(1)}, f32[2,128,128]{2,1,0:T(8,128)}, u32[]{:S(2)}) copy-start(f32[2,128,128]{2,1,0:T(8,128)} %inverse.5) | copy-start | bytes 393220
